TPU v7x, 8 devices: a whole 2x2x1 slice. The times are simulated.
8 devices in a mesh: dp: 1 (over z), tp: 8 (over x, y, core).
Axes of the slice: x: 2, y: 2, z: 1, core: 2. Of those that a mesh axis runs over, the one named last changes fastest.
Arguments:
- x: bfloat16 [64, 3072], P('dp')
- k_cache: bfloat16 [64, 4096, 8, 128], P('dp', None, 'tp')
- v_cache: bfloat16 [64, 4096, 8, 128], P('dp', None, 'tp')
- gain_a: bfloat16 [3072], replicated
- wq: bfloat16 [3072, 3072], P(None, 'tp')
- wo: bfloat16 [3072, 3072], P('tp')
- gain_m: bfloat16 [3072], replicated
- w_gate: bfloat16 [3072, 8192], P(None, 'tp')
- w_up: bfloat16 [3072, 8192], P(None, 'tp')
- w_down: bfloat16 [8192, 3072], P('tp')
Outputs:
- output: bfloat16 [64, 3072], P('dp')
All inputs are finite; a program needn't handle non-finite values.
Results may differ from a plain program's by a relative error of at most 0.017.
Values are sent between devices in bfloat16 or wider.
A program may use at most 2 GiB of HBM per device.

v0:
```python
import jax
import jax.numpy as jnp
from jax import lax
from jax.sharding import PartitionSpec as P

HEAD = 128
THETA = 10000


def normed(x, gain):
    wide = x.astype(jnp.float32)
    scale = lax.rsqrt(jnp.mean(wide * wide, -1, keepdims=True) + 1e-6)
    return (wide * scale * gain.astype(jnp.float32)).astype(jnp.bfloat16)


def turned(t, place, theta):
    half = t.shape[-1] // 2
    angle = place.astype(jnp.float32)[:, None] * theta ** (-jnp.arange(half, dtype=jnp.float32) / half)
    cos, sin = jnp.cos(angle)[:, None], jnp.sin(angle)[:, None]
    a, b = t[..., :half].astype(jnp.float32), t[..., half:].astype(jnp.float32)
    return jnp.concatenate([a * cos - b * sin, b * cos + a * sin], -1).astype(jnp.bfloat16)


def matmul(a, w):
    return jnp.dot(a, w, preferred_element_type=jnp.float32).astype(jnp.bfloat16)


def einsum(form, a, b):
    return jnp.einsum(form, a.astype(jnp.float32), b.astype(jnp.float32))


def seen_by(a, wq, k_cache, v_cache, head, theta):
    batch, cache, kv_heads = k_cache.shape[:3]
    place = jnp.full((batch,), cache - 1)
    q = turned(matmul(a, wq).reshape(batch, -1, head), place, theta).reshape(batch, kv_heads, -1, head)
    scores = einsum("bgsd,bugd->bgsu", q, k_cache) * head**-0.5
    weights = jax.nn.softmax(scores, -1).astype(jnp.bfloat16)
    return einsum("bgsu,bugd->bgsd", weights, v_cache).astype(jnp.bfloat16).reshape(batch, -1)


def hidden_of(b, w_gate, w_up):
    gate = jnp.dot(b, w_gate, preferred_element_type=jnp.float32)
    up = jnp.dot(b, w_up, preferred_element_type=jnp.float32)
    return (jax.nn.silu(gate) * up).astype(jnp.bfloat16)


def solution(mesh):
    def added(t, term):
        return (t.astype(jnp.float32) + lax.psum(term.astype(jnp.bfloat16), "tp").astype(jnp.float32)).astype(jnp.bfloat16)

    def step(x, k_cache, v_cache, gain_a, wq, wo, gain_m, w_gate, w_up, w_down):
        seen = seen_by(normed(x, gain_a), wq, k_cache, v_cache, HEAD, THETA)
        h = added(x, jnp.dot(seen, wo, preferred_element_type=jnp.float32))
        return added(h, jnp.dot(hidden_of(normed(h, gain_m), w_gate, w_up), w_down, preferred_element_type=jnp.float32))

    states, cache, columns, rows_of = P("dp", None), P("dp", None, "tp", None), P(None, "tp"), P("tp", None)
    return jax.shard_map(
        step,
        mesh=mesh,
        in_specs=(states, cache, cache, P(None), columns, rows_of, P(None), columns, columns, rows_of),
        out_specs=states,
        check_vma=False,
    )
```

profile of v0, /device:TPU:0, one launch (start us, length us, event | category | flops | bytes accessed | tf_op | source)
XLA Modules:
  0.0 174.4 jit_solution(8040045214403983640)
XLA Ops:
  6.5 0.0 copy-start
  6.5 0.0 all-reduce.3.cloned.1.call-start
  6.6 0.8 convert_element_type.66
  7.4 1.2 fusion.15
  8.6 2.4 %convolution_convert_fusion.2 = bf16[64,384]{1,0:T(8,128)(2,1)S(1)} fusion(bf16[3072,384]{1,0:T(8,128)(2,1)} %param.14, bf16[64,3072]{1,0:T(8,128)(2,1)} %param.10, f32[3072]{0:T(1024)S(1)} %convert_element_type.66, f32[64]{0:T(128)S(1)} %add_rsqrt_fusion.1), kind=kOutput, calls=%fused_computation.21 | convolution fusion | flops 151805952 | bytes 2814208 | tf_op jit(solution)/shard_map/dot_general | solution.py:25
  11.0 0.1 fusion.47
  11.2 0.1 pad_maximum_fusion
  11.3 27.7 %fusion.48 = (f32[64,3]{1,0:T(8,128)S(1)}, f32[64,3,4096]{2,1,0:T(4,128)}) fusion(bf16[64,4096,1,128]{3,1,2,0:T(8,128)(2,1)} %param.11, bf16[64,3,128]{2,0,1:T(8,128)(2,1)S(1)} %pad_maximum_fusion), kind=kOutput, calls=%fused_computation.58 | convolution fusion | flops 203689984 | bytes 70304512 | tf_op jit(solution)/shard_map/sub | solution.py:37
  39.0 0.0 copy-start.2
  39.0 0.0 copy-start.1
  39.0 24.0 %fusion.12 = bf16[64,3,128]{2,1,0:T(4,128)(2,1)S(1)} fusion(bf16[64,4096,1,128]{3,1,2,0:T(8,128)(2,1)} %param.12, f32[64,3,4096]{2,1,0:T(4,128)} %get-tuple-element.12, f32[64,3]{1,0:T(8,128)S(1)} %get-tuple-element.11), kind=kOutput, calls=%fused_computation.20 | convolution fusion | flops 202924032 | bytes 70304512 | tf_op jit(solution)/shard_map/bgsu,bugd->bgsd/dot_general | solution.py:29
  63.0 0.0 copy-done
  63.0 1.3 convolution_convert_fusion.1
  64.3 0.0 all-reduce.3.cloned.1.call-update
  64.3 0.0 all-reduce.5.cloned.1.call-start
  64.4 0.0 copy-done.2
  64.4 45.8 %all-reduce.3.cloned.1.call-done = bf16[64,3072]{1,0:T(8,128)(2,1)} async-done(((bf16[64,3072]{1,0:T(8,128)(2,1)}), bf16[64,3072]{1,0:T(8,128)(2,1)}) %all-reduce.3.cloned.1.call-update) | async-done | bytes 393232 | tf_op jit(solution)/shard_map/psum | solution.py:49
  110.2 0.0 copy-done.1
  110.2 1.2 fusion.19
  111.5 4.0 %fusion.34 = f32[64,1024]{1,0:T(8,128)S(1)} fusion(bf16[3072,1024]{1,0:T(8,128)(2,1)} %param.17, bf16[64,3072]{1,0:T(8,128)(2,1)S(1)} %get-tuple-element.6, f32[3072]{0:T(1024)S(1)} %convert_element_type.77, f32[64]{0:T(128)S(1)} %add_rsqrt_fusion), kind=kOutput, calls=%fused_computation.42 | convolution fusion | flops 403439616 | bytes 6959360 | tf_op jit(solution)/shard_map/dot_general | solution.py:42
  115.5 7.7 %convolution_convert_fusion = bf16[64,3072]{1,0:T(8,128)(2,1)} fusion(bf16[1024,3072]{1,0:T(8,128)(2,1)} %param.19, bf16[3072,1024]{1,0:T(8,128)(2,1)} %param.18, f32[64,1024]{1,0:T(8,128)S(1)} %fusion.34, bf16[64,3072]{1,0:T(8,128)(2,1)S(1)} %get-tuple-element.6, f32[3072]{0:T(1024)S(1)} %convert_element_type.77, f32[64]{0:T(128)S(1)} %add_rsqrt_fusion), kind=kOutput, calls=%fused_computation.9 | convolution fusion | flops 806682624 | bytes 13644032 | tf_op jit(solution)/shard_map/dot_general | solution.py:54
  123.3 0.0 all-reduce.5.cloned.1.call-update
  123.3 42.4 %all-reduce.5.cloned.1.call-done = bf16[64,3072]{1,0:T(8,128)(2,1)} async-done(((bf16[64,3072]{1,0:T(8,128)(2,1)}), bf16[64,3072]{1,0:T(8,128)(2,1)}) %all-reduce.5.cloned.1.call-update) | async-done | bytes 393232 | tf_op jit(solution)/shard_map/psum | solution.py:49
  165.7 1.8 %fusion.22 = bf16[64,3072]{1,0:T(8,128)(2,1)} fusion(bf16[64,3072]{1,0:T(8,128)(2,1)S(1)} %get-tuple-element.6, bf16[64,3072]{1,0:T(8,128)(2,1)} %all-reduce.5.cloned.1.call-done), kind=kLoop, calls=%fused_computation.29 | loop fusion | flops 786432 | bytes 1179648 | tf_op jit(solution)/shard_map/convert_element_type | solution.py:49
  (6 shorter events, 0.1 us)
Async XLA Ops:
  6.5 56.5 %copy-start = (bf16[384,3072]{1,0:T(8,128)(2,1)S(1)}, bf16[384,3072]{1,0:T(8,128)(2,1)}, u32[]{:S(2)}) copy-start(bf16[384,3072]{1,0:T(8,128)(2,1)} %param.15) | copy-start | bytes 7077892
  6.5 103.7 %all-reduce.3.cloned.1.call-start = ((), (), s32[]{:S(2)}) async-start(), calls=%async_computation | async-start | bytes 786432 | tf_op jit(solution)/shard_map/psum | solution.py:49
  39.0 25.4 %copy-start.2 = (bf16[3072]{0:T(1024)(128)(2,1)S(1)}, bf16[3072]{0:T(1024)(128)(2,1)}, u32[]{:S(2)}) copy-start(bf16[3072]{0:T(1024)(128)(2,1)} %param.16) | copy-start | bytes 18436
  39.0 71.2 %copy-start.1 = (bf16[64,3072]{1,0:T(8,128)(2,1)S(1)}, bf16[64,3072]{1,0:T(8,128)(2,1)}, u32[]{:S(2)}) copy-start(bf16[64,3072]{1,0:T(8,128)(2,1)} %param.10) | copy-start | bytes 1179652
  64.3 101.4 %all-reduce.5.cloned.1.call-start = ((), (), s32[]{:S(2)}) async-start(), calls=%async_computation.1 | async-start | bytes 786432 | tf_op jit(solution)/shard_map/psum | solution.py:49
Sparse Core Ops, SparseCore 0:
  64.5 45.7 all-reduce.2
  123.4 42.2 all-reduce.4
where the time goes:
time: 175 us; the launch traced here: 174 us
  waiting for transfers between devices  88.3 us (50%)
  matrix products  67.1 us (38%)
  between operations  13.5 us (8%)
  other arithmetic  5.28 us (3%)
    psum x2, waiting for transfers between devices, added(): lax.psum(term.astype(jnp.bfloat16), 'tp').astype(jnp.float32)  88.3 us
    sub x1, matrix products, seen_by(): weights = jax.nn.softmax(scores, -1).astype(jnp.bfloat16)  27.7 us
    dot_general x1, matrix products, einsum(): return jnp.einsum(form, a.astype(jnp.float32), b.astype(jnp.float32))  24 us
    dot_general x1, matrix products, step(): jnp.dot(hidden_of(normed(h, gain_m), w_gate, w_up), w_down, preferred_ele...  7.72 us
    dot_general x1, matrix products, hidden_of(): gate = jnp.dot(b, w_gate, preferred_element_type=jnp.float32)  4.05 us
  transfers between devices with their start and end apart: 2, of which 2 were waited for; matrix products, arithmetic and copies ran while one was open for 0% of the time, Pallas kernels for 0%

commit v1 on v0

v1 whole, which is shorter than its diff:
```python
import functools, math
import jax, jax.numpy as jnp, numpy as np
from jax import lax
from jax.experimental import pallas as pl
from jax.experimental.pallas import tpu as pltpu
from jax.sharding import PartitionSpec as P

HEAD=128; THETA=10000; D=3072; B=64; U=4096; Q=4; G=B//Q; NS=3; UC=512
ANY=pl.BlockSpec(memory_space=pl.ANY); VM=pl.BlockSpec(memory_space=pltpu.VMEM)

def normed(x, gain):
    w = x.astype(jnp.float32)
    s = lax.rsqrt(jnp.mean(w*w, -1, keepdims=True)+1e-6)
    return (w*s*gain.astype(jnp.float32)).astype(jnp.bfloat16)

def rot_tables():
    half=HEAD//2
    ang=(U-1)*THETA**(-np.arange(half,dtype=np.float64)/half)
    c,s=np.cos(ang),np.sin(ang)
    return np.concatenate([c,c])[None].astype(np.float32), np.concatenate([-s,s])[None].astype(np.float32)

def att_kernel(x_ref, ga_ref, cos_ref, sin_ref, wq_hbm, wo_hbm, k_hbm, v_hbm, out_ref,
               kbuf, vbuf, wq, wo, qblk, sbuf, oall, ksem, vsem, wsem):
    def kcopy(g, slot):
        return pltpu.make_async_copy(k_hbm.at[pl.ds(g*Q,Q)], kbuf.at[slot], ksem.at[slot])
    def vcopy(g, slot):
        return pltpu.make_async_copy(v_hbm.at[pl.ds(g*Q,Q)], vbuf.at[slot], vsem.at[slot])
    wqc=pltpu.make_async_copy(wq_hbm, wq, wsem.at[0]); wqc.start()
    kcopy(0,0).start(); kcopy(1,1).start(); vcopy(0,0).start(); kcopy(2,2).start(); vcopy(1,1).start()
    woc=pltpu.make_async_copy(wo_hbm, wo, wsem.at[1]); woc.start()
    a = normed(x_ref[...], ga_ref[...])
    wqc.wait()
    q = jnp.dot(a, wq[...], preferred_element_type=jnp.float32).astype(jnp.bfloat16).astype(jnp.float32)
    C, S = cos_ref[...], sin_ref[...]
    r = lax.broadcasted_iota(jnp.int32,(16*G,B),0); s = lax.broadcasted_iota(jnp.int32,(16*G,B),1)
    rr, gg = r%16, r//16
    qa = jnp.zeros((16*G,HEAD),jnp.float32)
    for h in range(3):
        qh=q[:,h*HEAD:(h+1)*HEAD]
        t=(qh*C+pltpu.roll(qh,HEAD//2,1)*S).astype(jnp.bfloat16)
        E=((s==gg*Q+rr-h*Q)&(rr>=h*Q)&(rr<(h+1)*Q)).astype(jnp.bfloat16)
        qa += jnp.dot(E,t,preferred_element_type=jnp.float32)
    rowl=lax.broadcasted_iota(jnp.int32,(16*G,HEAD),0)%Q
    for sl in range(Q):
        qblk[:,sl*HEAD:(sl+1)*HEAD]=jnp.where(rowl==sl,qa,0.).astype(jnp.bfloat16)
    rowo=lax.broadcasted_iota(jnp.int32,(16,HEAD),0)%Q

    def scores(g, kslot, sslot):
        ql=qblk[pl.ds(pl.multiple_of(g*16,16),16),:]
        for c in range(U//UC):
            kc=jnp.concatenate([kbuf[kslot,i,c*UC:(c+1)*UC,:] for i in range(Q)],axis=1)
            sbuf[sslot,:,c*UC:(c+1)*UC]=lax.dot_general(ql,kc,(((1,),(1,)),((),())),preferred_element_type=jnp.float32)
    def attend(g, vslot, sslot):
        sc=sbuf[sslot]
        m=jnp.max(sc,axis=1,keepdims=True)
        p=jnp.exp2((sc-m)*(HEAD**-0.5*math.log2(math.e)))
        l=jnp.sum(p,axis=1,keepdims=True)
        w=(p*(1.0/l)).astype(jnp.bfloat16)
        o=jnp.zeros((16,Q*HEAD),jnp.float32)
        for c in range(U//UC):
            vc=jnp.concatenate([vbuf[vslot,i,c*UC:(c+1)*UC,:] for i in range(Q)],axis=1)
            o=o+jnp.dot(w[:,c*UC:(c+1)*UC],vc,preferred_element_type=jnp.float32)
        t=jnp.zeros((16,HEAD),jnp.float32)
        for i in range(Q):
            t=jnp.where(rowo==i,o[:,i*HEAD:(i+1)*HEAD],t)
        oall[pl.ds(pl.multiple_of(g*16,16),16),:]=t.astype(jnp.bfloat16)

    kcopy(0,0).wait()
    scores(0,0,0)
    def body(g, _):
        kn=lax.rem(g+1,NS); vn=lax.rem(g,NS)
        kcopy(g+1,kn).wait(); vcopy(g,vn).wait()
        @pl.when(g+3<G)
        def _(): kcopy(g+3,vn).start()
        @pl.when(g+2<G)
        def _(): vcopy(g+2,lax.rem(g+2,NS)).start()
        scores(g+1,kn,lax.rem(g+1,2))
        attend(g,vn,lax.rem(g,2))
        return 0
    lax.fori_loop(0,G-1,body,0)
    vcopy(G-1,(G-1)%NS).wait()
    attend(G-1,(G-1)%NS,(G-1)%2)
    woc.wait()
    rT = lax.broadcasted_iota(jnp.int32,(B,16*G),1); sT = lax.broadcasted_iota(jnp.int32,(B,16*G),0)
    rr, gg = rT%16, rT//16
    acc=jnp.zeros((B,D),jnp.float32)
    seen=[]
    for h in range(3):
        E=((sT==gg*Q+rr-h*Q)&(rr>=h*Q)&(rr<(h+1)*Q)).astype(jnp.bfloat16)
        seen.append(jnp.dot(E,oall[...],preferred_element_type=jnp.float32).astype(jnp.bfloat16))
    out_ref[...]=jnp.dot(jnp.concatenate(seen,axis=1),wo[...],preferred_element_type=jnp.float32).astype(jnp.bfloat16)

def attention_partial(x, k, v, ga, wq, wo):
    C,S=rot_tables()
    return pl.pallas_call(att_kernel,
        out_shape=jax.ShapeDtypeStruct((B,D),jnp.bfloat16),
        in_specs=[VM,VM,VM,VM,ANY,ANY,ANY,ANY], out_specs=VM,
        scratch_shapes=[pltpu.VMEM((NS,Q,U,HEAD),jnp.bfloat16),pltpu.VMEM((NS,Q,U,HEAD),jnp.bfloat16),
            pltpu.VMEM((D,384),jnp.bfloat16),pltpu.VMEM((384,D),jnp.bfloat16),pltpu.VMEM((16*G,Q*HEAD),jnp.bfloat16),
            pltpu.VMEM((2,16,U),jnp.float32),pltpu.VMEM((16*G,HEAD),jnp.bfloat16),
            pltpu.SemaphoreType.DMA((NS,)),pltpu.SemaphoreType.DMA((NS,)),pltpu.SemaphoreType.DMA((2,))],
        compiler_params=pltpu.CompilerParams(vmem_limit_bytes=60*2**20),
        name="att",
    )(x,ga[None],jnp.asarray(C),jnp.asarray(S),wq,wo,k.reshape(B,U,HEAD),v.reshape(B,U,HEAD))

def hidden_of(b, w_gate, w_up):
    gate = jnp.dot(b, w_gate, preferred_element_type=jnp.float32)
    up = jnp.dot(b, w_up, preferred_element_type=jnp.float32)
    return (jax.nn.silu(gate) * up).astype(jnp.bfloat16)

def solution(mesh):
    def added(t, term):
        return (t.astype(jnp.float32) + lax.psum(term.astype(jnp.bfloat16), "tp").astype(jnp.float32)).astype(jnp.bfloat16)
    def step(x, k_cache, v_cache, gain_a, wq, wo, gain_m, w_gate, w_up, w_down):
        h = added(x, attention_partial(x,k_cache,v_cache,gain_a,wq,wo))
        return added(h, jnp.dot(hidden_of(normed(h, gain_m), w_gate, w_up), w_down, preferred_element_type=jnp.float32))
    states, cache, columns, rows_of = P("dp", None), P("dp", None, "tp", None), P(None, "tp"), P("tp", None)
    return jax.shard_map(step, mesh=mesh,
        in_specs=(states, cache, cache, P(None), columns, rows_of, P(None), columns, columns, rows_of),
        out_specs=states, check_vma=False)
```

time: 175 us -> 164 us (0.937)
  matrix products: 67.1 us -> 11.8 us
  Pallas kernels: 0 us -> 45.4 us
  other arithmetic: 5.28 us -> 3.08 us
    pallas_call x0 -> x1, Pallas kernels: none -> 45.4 us  [attention_partial(): pl.pallas_call(att_kernel, out_shape=jax.ShapeDtypeStruct((B, D), jnp.bfl...]
    sub x1 -> x0, matrix products: 27.7 us -> none  [seen_by(): weights = jax.nn.softmax(scores, -1).astype(jnp.bfloat16)]
    dot_general x3 -> x0, matrix products: 27.6 us -> none  [the longest x1 24 us: einsum(): return jnp.einsum(form, a.astype(jnp.float32), b.astype(jnp.float32))]
where the time goes in v1:
time: 164 us; the launch traced here: 163 us
  waiting for transfers between devices  88.3 us (54%)
  Pallas kernels  45.4 us (28%)
  between operations  13.4 us (8%)
  matrix products  11.8 us (7%)
  other arithmetic  3.08 us (2%)
    psum x2, waiting for transfers between devices, added(): lax.psum(term.astype(jnp.bfloat16), 'tp').astype(jnp.float32)  88.3 us
    pallas_call x1, Pallas kernels, attention_partial(): pl.pallas_call(att_kernel, out_shape=jax.ShapeDtypeStruct((B, D), jnp.bfl...  45.4 us
    dot_general x1, matrix products, step(): jnp.dot(hidden_of(normed(h, gain_m), w_gate, w_up), w_down, preferred_ele...  7.72 us
    dot_general x1, matrix products, hidden_of(): gate = jnp.dot(b, w_gate, preferred_element_type=jnp.float32)  4.05 us
  transfers between devices with their start and end apart: 2, of which 2 were waited for; matrix products, arithmetic and copies ran while one was open for 0% of the time, Pallas kernels for 0%

profile of v1, /device:TPU:0, one launch (start us, length us, event | category | flops | bytes accessed | tf_op | source)
XLA Modules:
  0.0 163.4 jit_solution(16354128020887672216)
XLA Ops:
  6.5 0.0 all-reduce.3.cloned.1.call-start
  6.5 1.3 broadcast_in_dim.2.ga_ref
  7.8 0.0 copy-start.1
  7.8 0.0 copy-start
  7.8 45.4 %att.1 = bf16[64,3072]{1,0:T(8,128)(2,1)} custom-call(bf16[64,3072]{1,0:T(8,128)(2,1)} %x_ref.1, bf16[1,3072]{1,0:T(2,128)(2,1)} %broadcast_in_dim.2.ga_ref, f32[1,128]{1,0:T(1,128)} %constant.14.clone.cos_ref, f32[1,128]{1,0:T(1,128)} %constant.15.clone.sin_ref, bf16[3072,384]{1,0:T(8,128)(2,1)} %wq_hbm.1, bf16[384,3072]{1,0:T(8,128)(2,1)} %wo_hbm.1, ...), custom_call_target="tpu_custom_call" | custom-call | tf_op jit(solution)/shard_map/att/pallas_call | solution.py:95
  53.2 0.0 all-reduce.3.cloned.1.call-update
  53.3 0.0 all-reduce.5.cloned.1.call-start
  53.3 0.0 copy-done.1
  53.3 45.9 %all-reduce.3.cloned.1.call-done = bf16[64,3072]{1,0:T(8,128)(2,1)} async-done(((bf16[64,3072]{1,0:T(8,128)(2,1)}), bf16[64,3072]{1,0:T(8,128)(2,1)}) %all-reduce.3.cloned.1.call-update) | async-done | bytes 393232 | tf_op jit(solution)/shard_map/psum | solution.py:113
  99.2 0.0 copy-done
  99.2 1.2 fusion.1
  100.5 4.0 %fusion.13 = f32[64,1024]{1,0:T(8,128)S(1)} fusion(bf16[3072,1024]{1,0:T(8,128)(2,1)} %param.19, bf16[64,3072]{1,0:T(8,128)(2,1)S(1)} %get-tuple-element.6, f32[3072]{0:T(1024)S(1)} %convert_element_type.35, f32[64]{0:T(128)S(1)} %add_rsqrt_fusion), kind=kOutput, calls=%fused_computation.17 | convolution fusion | flops 403439616 | bytes 6959360 | tf_op jit(solution)/shard_map/dot_general | solution.py:107
  104.5 7.7 %convolution_convert_fusion = bf16[64,3072]{1,0:T(8,128)(2,1)} fusion(bf16[1024,3072]{1,0:T(8,128)(2,1)} %param.21, bf16[3072,1024]{1,0:T(8,128)(2,1)} %param.20, f32[64,1024]{1,0:T(8,128)S(1)} %fusion.13, bf16[64,3072]{1,0:T(8,128)(2,1)S(1)} %get-tuple-element.6, f32[3072]{0:T(1024)S(1)} %convert_element_type.35, f32[64]{0:T(128)S(1)} %add_rsqrt_fusion), kind=kOutput, calls=%fused_computation | convolution fusion | flops 806682624 | bytes 13644032 | tf_op jit(solution)/shard_map/dot_general | solution.py:116
  112.2 0.0 all-reduce.5.cloned.1.call-update
  112.3 42.4 %all-reduce.5.cloned.1.call-done = bf16[64,3072]{1,0:T(8,128)(2,1)} async-done(((bf16[64,3072]{1,0:T(8,128)(2,1)}), bf16[64,3072]{1,0:T(8,128)(2,1)}) %all-reduce.5.cloned.1.call-update) | async-done | bytes 393232 | tf_op jit(solution)/shard_map/psum | solution.py:113
  154.7 1.8 %fusion.4 = bf16[64,3072]{1,0:T(8,128)(2,1)} fusion(bf16[64,3072]{1,0:T(8,128)(2,1)S(1)} %get-tuple-element.6, bf16[64,3072]{1,0:T(8,128)(2,1)} %all-reduce.5.cloned.1.call-done), kind=kLoop, calls=%fused_computation.9 | loop fusion | flops 786432 | bytes 1179648 | tf_op jit(solution)/shard_map/convert_element_type | solution.py:113
  (2 shorter events, 0.0 us)
Async XLA Ops:
  6.5 92.7 %all-reduce.3.cloned.1.call-start = ((), (), s32[]{:S(2)}) async-start(), calls=%async_computation | async-start | bytes 786432 | tf_op jit(solution)/shard_map/psum | solution.py:113
  7.8 45.5 %copy-start.1 = (bf16[3072]{0:T(1024)(128)(2,1)S(1)}, bf16[3072]{0:T(1024)(128)(2,1)}, u32[]{:S(2)}) copy-start(bf16[3072]{0:T(1024)(128)(2,1)} %param.18) | copy-start | bytes 18436
  7.8 91.4 %copy-start = (bf16[64,3072]{1,0:T(8,128)(2,1)S(1)}, bf16[64,3072]{1,0:T(8,128)(2,1)}, u32[]{:S(2)}) copy-start(bf16[64,3072]{1,0:T(8,128)(2,1)} %x_ref.1) | copy-start | bytes 1179652
  53.3 101.4 %all-reduce.5.cloned.1.call-start = ((), (), s32[]{:S(2)}) async-start(), calls=%async_computation.1 | async-start | bytes 786432 | tf_op jit(solution)/shard_map/psum | solution.py:113
Sparse Core Ops, SparseCore 0:
  53.4 45.7 all-reduce.2
  112.4 42.2 all-reduce.4

commit v2 on v0

v2 whole, which is shorter than its diff:
```python
import math

import jax
import jax.numpy as jnp
import numpy as np
from jax import lax
from jax.experimental import pallas as pl
from jax.experimental.pallas import tpu as pltpu
from jax.sharding import PartitionSpec as P

HEAD = 128
THETA = 10000
D = 3072
B = 64
U = 4096
Q = 4
G = B // Q
NS = 3
UC = 512
N = 8
W = D // N
HID = 1024
CHUNKS = ((0, 12), (12, 4))
REDUCE_AT = 13
QUERIES = 3
F32, BF16 = jnp.float32, jnp.bfloat16
MESH = pl.DeviceIdType.MESH


def rotary_tables():
    half = HEAD // 2
    angle = (U - 1) * THETA ** (-np.arange(half, dtype=np.float64) / half)
    cos, sin = np.cos(angle), np.sin(angle)
    return np.concatenate([cos, cos])[None].astype(np.float32), np.concatenate([-sin, sin])[None].astype(np.float32)


def row(gain):
    return jnp.concatenate([gain[i : i + 1] for i in range(gain.shape[0])], axis=1)


def dot(a, b):
    return jnp.dot(a, b, preferred_element_type=F32)


def layer(x_ref, ga_ref, gm_ref, cos_ref, sin_ref, wq_hbm, wo_hbm, wg_hbm, wu_hbm, wd_hbm, k_hbm, v_hbm, out_ref,
          kbuf, vbuf, wq, wo, wg, wu, wd, qblk, sbuf, oall, bbuf, hid, *rest):
    nc = len(CHUNKS)
    own, part1, part2, recv1, recv2, hbuf, ybuf = (rest[i * nc : (i + 1) * nc] for i in range(7))
    ksem, vsem, wsem, send_sem, recv_sem = rest[7 * nc :]
    me = lax.axis_index("tp")

    def at(d):
        return lax.rem(me + d, N)

    barrier = pltpu.get_barrier_semaphore()
    for d in range(1, N):
        pl.semaphore_signal(barrier, inc=1, device_id={"tp": at(d)}, device_id_type=MESH)

    def kcopy(g, slot):
        return pltpu.make_async_copy(k_hbm.at[pl.ds(g * Q, Q)], kbuf.at[slot], ksem.at[slot])

    def vcopy(g, slot):
        return pltpu.make_async_copy(v_hbm.at[pl.ds(g * Q, Q)], vbuf.at[slot], vsem.at[slot])

    half = HID // 2
    loads = {"wq": pltpu.make_async_copy(wq_hbm, wq, wsem.at[0]), "wo": pltpu.make_async_copy(wo_hbm, wo, wsem.at[1])}
    for n in range(2):
        cols = pl.ds(n * half, half)
        loads["wg", n] = pltpu.make_async_copy(wg_hbm.at[:, cols], wg.at[:, cols], wsem.at[2 + n])
        loads["wu", n] = pltpu.make_async_copy(wu_hbm.at[:, cols], wu.at[:, cols], wsem.at[4 + n])
    loads["wd"] = pltpu.make_async_copy(wd_hbm, wd, wsem.at[6])

    def scatter(c, stage, src, dst):
        return [pltpu.make_async_remote_copy(src.at[at(d)], dst.at[d], send_sem.at[c, stage, d], recv_sem.at[c, stage, d],
                                             device_id={"tp": at(d)}, device_id_type=MESH) for d in range(1, N)]

    def gather(c, stage, buf):
        return [pltpu.make_async_remote_copy(buf.at[me], buf.at[me], send_sem.at[c, stage, d], recv_sem.at[c, stage, d],
                                             device_id={"tp": at(d)}, device_id_type=MESH) for d in range(1, N)]

    def start(copies):
        for copy in copies:
            copy.start()

    def arrived(copies):
        for copy in copies:
            copy.wait_recv()

    def rows_of(c):
        return CHUNKS[c][0] * Q, CHUNKS[c][1] * Q

    loads["wq"].start()
    kcopy(0, 0).start()
    kcopy(1, 1).start()
    vcopy(0, 0).start()
    kcopy(2, 2).start()
    vcopy(1, 1).start()
    loads["wo"].start()
    wide = x_ref[...].astype(F32)
    scale = lax.rsqrt(jnp.mean(wide * wide, -1, keepdims=True) + 1e-6)
    a = (wide * scale * row(ga_ref[...].astype(F32))).astype(BF16)
    loads["wq"].wait()
    q = dot(a, wq[...]).astype(BF16).astype(F32)

    def picks(shape, row_axis, first):
        r = lax.broadcasted_iota(jnp.int32, shape, row_axis)
        s = lax.broadcasted_iota(jnp.int32, shape, 1 - row_axis) + first * Q
        rr = r % 16
        gg = r // 16 + first
        return [((s == gg * Q + rr - h * Q) & (rr >= h * Q) & (rr < (h + 1) * Q)).astype(BF16) for h in range(QUERIES)]

    qa = jnp.zeros((16 * G, HEAD), F32)
    for h, pick in enumerate(picks((16 * G, B), 0, 0)):
        qh = q[:, h * HEAD : (h + 1) * HEAD]
        qa += dot(pick, (qh * cos_ref[...] + pltpu.roll(qh, HEAD // 2, 1) * sin_ref[...]).astype(BF16))
    block = lax.broadcasted_iota(jnp.int32, (16 * G, HEAD), 0) % Q
    for i in range(Q):
        qblk[:, i * HEAD : (i + 1) * HEAD] = jnp.where(block == i, qa, 0.0).astype(BF16)
    block = lax.broadcasted_iota(jnp.int32, (16, HEAD), 0) % Q

    def quad_rows(g):
        return pl.ds(pl.multiple_of(g * 16, 16), 16)

    def scores(g, slot, to):
        ql = qblk[quad_rows(g), :]
        for u in range(0, U, UC):
            kc = jnp.concatenate([kbuf[slot, i, u : u + UC, :] for i in range(Q)], axis=1)
            sbuf[to, :, u : u + UC] = lax.dot_general(ql, kc, (((1,), (1,)), ((), ())), preferred_element_type=F32)

    def attend(g, slot, of):
        s = sbuf[of]
        p = jnp.exp2((s - jnp.max(s, axis=1, keepdims=True)) * (HEAD**-0.5 * math.log2(math.e)))
        w = (p * (1.0 / jnp.sum(p, axis=1, keepdims=True))).astype(BF16)
        o = jnp.zeros((16, Q * HEAD), F32)
        for u in range(0, U, UC):
            o += dot(w[:, u : u + UC], jnp.concatenate([vbuf[slot, i, u : u + UC, :] for i in range(Q)], axis=1))
        t = jnp.zeros((16, HEAD), F32)
        for i in range(Q):
            t = jnp.where(block == i, o[:, i * HEAD : (i + 1) * HEAD], t)
        oall[quad_rows(g), :] = t.astype(BF16)

    def terms(c, a, w_ref, part):
        for n in range(4):
            t = dot(a, w_ref[:, n * 2 * W : (n + 1) * 2 * W])
            for j in range(2):
                own[c][2 * n + j] = t[:, j * W : (j + 1) * W]
                part[2 * n + j] = t[:, j * W : (j + 1) * W].astype(BF16)

    def finish(c):
        first, quads = CHUNKS[c]
        o = oall[first * 16 : (first + quads) * 16, :]
        seen = [dot(pick, o).astype(BF16) for pick in picks((quads * Q, quads * 16), 1, first)]
        if c == 0:
            loads["wo"].wait()
            pl.semaphore_wait(barrier, N - 1)
        terms(c, jnp.concatenate(seen, axis=1), wo, part1[c])
        start(scatter(c, 0, part1[c], recv1[c]))

    def summed(c, stage, part, recv):
        arrived(scatter(c, stage, part, recv))
        t = own[c][me]
        for d in range(1, N):
            t += recv[d].astype(F32)
        return t

    def reduce1(c):
        first, rows = rows_of(c)
        t = summed(c, 0, part1[c], recv1[c])
        mine = x_ref[first : first + rows, pl.ds(pl.multiple_of(me * W, 128), W)].astype(F32)
        hbuf[c][me] = (mine + t).astype(BF16)
        start(gather(c, 1, hbuf[c]))

    def reduce2(c):
        t = summed(c, 2, part2[c], recv2[c])
        ybuf[c][me] = (hbuf[c][me].astype(F32) + t).astype(BF16)
        start(gather(c, 3, ybuf[c]))

    def norm2(c):
        first, rows = rows_of(c)
        arrived(gather(c, 1, hbuf[c]))
        squares = jnp.zeros((rows, 1), F32)
        for j in range(N):
            t = hbuf[c][j].astype(F32)
            squares += jnp.sum(t * t, -1, keepdims=True)
        scale = lax.rsqrt(squares * (1.0 / D) + 1e-6)
        gain = row(gm_ref[...].astype(F32))
        for j in range(N):
            bbuf[first : first + rows, j * W : (j + 1) * W] = (hbuf[c][j].astype(F32) * scale * gain[:, j * W : (j + 1) * W]).astype(BF16)

    def hidden(c, n):
        first, rows = rows_of(c)
        if c == 0:
            loads["wg", n].wait()
            loads["wu", n].wait()
        b = bbuf[first : first + rows, :]
        gate = dot(b, wg[:, n * half : (n + 1) * half])
        up = dot(b, wu[:, n * half : (n + 1) * half])
        hid[first : first + rows, n * half : (n + 1) * half] = (jax.nn.silu(gate) * up).astype(BF16)

    def down(c):
        first, rows = rows_of(c)
        if c == 0:
            loads["wd"].wait()
        terms(c, hid[first : first + rows, :], wd, part2[c])
        start(scatter(c, 2, part2[c], recv2[c]))

    kcopy(0, 0).wait()
    scores(0, 0, 0)

    def body(g, _):
        kslot, vslot = lax.rem(g + 1, NS), lax.rem(g, NS)
        kcopy(g + 1, kslot).wait()
        vcopy(g, vslot).wait()

        @pl.when(g + 3 < G)
        def _():
            kcopy(g + 3, vslot).start()

        @pl.when(g + 2 < G)
        def _():
            vcopy(g + 2, lax.rem(g + 2, NS)).start()

        scores(g + 1, kslot, lax.rem(g + 1, 2))
        attend(g, vslot, lax.rem(g, 2))

        @pl.when(g == CHUNKS[0][1] - 1)
        def _():
            finish(0)

        @pl.when(g == REDUCE_AT)
        def _():
            reduce1(0)

        return 0

    lax.fori_loop(0, G - 1, body, 0)
    vcopy(G - 1, (G - 1) % NS).wait()
    for n in range(2):
        loads["wg", n].start()
        loads["wu", n].start()
    loads["wd"].start()
    attend(G - 1, (G - 1) % NS, (G - 1) % 2)
    finish(1)
    norm2(0)
    hidden(0, 0)
    reduce1(1)
    hidden(0, 1)
    down(0)
    norm2(1)
    hidden(1, 0)
    hidden(1, 1)
    down(1)
    reduce2(0)
    reduce2(1)
    for c in range(nc):
        first, rows = rows_of(c)
        arrived(gather(c, 3, ybuf[c]))
        for j in range(N):
            out_ref[first : first + rows, j * W : (j + 1) * W] = ybuf[c][j]
    for c in range(nc):
        for copies in (scatter(c, 0, part1[c], recv1[c]), gather(c, 1, hbuf[c]), scatter(c, 2, part2[c], recv2[c]), gather(c, 3, ybuf[c])):
            for copy in copies:
                copy.wait_send()


def solution(mesh):
    any_, vmem = pl.BlockSpec(memory_space=pl.ANY), pl.BlockSpec(memory_space=pltpu.VMEM)

    def step(x, k_cache, v_cache, gain_a, wq, wo, gain_m, w_gate, w_up, w_down):
        cos, sin = rotary_tables()

        def blocks(dtype, lead=N):
            return [pltpu.VMEM((lead, quads * Q, W), dtype) for _, quads in CHUNKS]

        nc = len(CHUNKS)
        return pl.pallas_call(
            layer,
            out_shape=jax.ShapeDtypeStruct((B, D), BF16),
            in_specs=[vmem] * 5 + [any_] * 7,
            out_specs=vmem,
            scratch_shapes=[
                pltpu.VMEM((NS, Q, U, HEAD), BF16),
                pltpu.VMEM((NS, Q, U, HEAD), BF16),
                pltpu.VMEM((D, QUERIES * HEAD), BF16),
                pltpu.VMEM((QUERIES * HEAD, D), BF16),
                pltpu.VMEM((D, HID), BF16),
                pltpu.VMEM((D, HID), BF16),
                pltpu.VMEM((HID, D), BF16),
                pltpu.VMEM((16 * G, Q * HEAD), BF16),
                pltpu.VMEM((2, 16, U), F32),
                pltpu.VMEM((16 * G, HEAD), BF16),
                pltpu.VMEM((B, D), BF16),
                pltpu.VMEM((B, HID), BF16),
                *blocks(F32), *blocks(BF16), *blocks(BF16), *blocks(BF16), *blocks(BF16), *blocks(BF16), *blocks(BF16),
                pltpu.SemaphoreType.DMA((NS,)),
                pltpu.SemaphoreType.DMA((NS,)),
                pltpu.SemaphoreType.DMA((7,)),
                pltpu.SemaphoreType.DMA((nc, 4, N)),
                pltpu.SemaphoreType.DMA((nc, 4, N)),
            ],
            compiler_params=pltpu.CompilerParams(collective_id=0, has_side_effects=True, vmem_limit_bytes=62 * 2**20),
            name="layer",
        )(x, gain_a.reshape(-1, 128), gain_m.reshape(-1, 128), jnp.asarray(cos), jnp.asarray(sin), wq, wo, w_gate, w_up, w_down,
          k_cache.reshape(B, U, HEAD), v_cache.reshape(B, U, HEAD))

    states, cache, columns, rows_of = P("dp", None), P("dp", None, "tp", None), P(None, "tp"), P("tp", None)
    return jax.shard_map(
        step,
        mesh=mesh,
        in_specs=(states, cache, cache, P(None), columns, rows_of, P(None), columns, columns, rows_of),
        out_specs=states,
        check_vma=False,
    )
```

time: 175 us -> 68.9 us (0.39)
  waiting for transfers between devices: 88.3 us -> 0 us
  matrix products: 67.1 us -> 0 us
  Pallas kernels: 0 us -> 67 us
  between operations: 13.5 us -> 0.01 us
  other arithmetic: 5.28 us -> 0 us
    psum x2 -> x0, waiting for transfers between devices: 88.3 us -> none  [added(): lax.psum(term.astype(jnp.bfloat16), 'tp').astype(jnp.float32)]
    pallas_call x0 -> x1, Pallas kernels: none -> 67 us  [step(): pl.pallas_call(layer, out_shape=jax.ShapeDtypeStruct((B, D), BF16), in_sp...]
    dot_general x5 -> x0, matrix products: 39.4 us -> none  [the longest x1 24 us: einsum(): return jnp.einsum(form, a.astype(jnp.float32), b.astype(jnp.float32))]
    sub x1 -> x0, matrix products: 27.7 us -> none  [seen_by(): weights = jax.nn.softmax(scores, -1).astype(jnp.bfloat16)]
    convert_element_type x3 -> x0, other arithmetic: 2.69 us -> none  [the longest x1 1.83 us: added(): (t.astype(jnp.float32) + lax.psum(term.astype(jnp.bfloat16), 'tp').astype...]
    reduce_sum x2 -> x0, other arithmetic: 2.41 us -> none  [normed(): scale = lax.rsqrt(jnp.mean(wide * wide, -1, keepdims=True) + 1e-06)]
    unnamed x6 -> x1, local copies, waits for them, and re-layouts: 0.01 us -> 1.77 us
  transfers between devices with their start and end apart: 2 -> 0, of which waited for: 2 -> 0; matrix products, arithmetic and copies ran while one was open for 0% -> 0% of each run, Pallas kernels for 0% -> 0%
where the time goes in v2:
time: 68.9 us; the launch traced here: 68.8 us
  Pallas kernels  67 us (97%)
  local copies, waits for them, and re-layouts  1.77 us (3%)
    pallas_call x1, Pallas kernels, step(): pl.pallas_call(layer, out_shape=jax.ShapeDtypeStruct((B, D), BF16), in_sp...  67 us
    unnamed x1, local copies, waits for them, and re-layouts  1.77 us

profile of v2, /device:TPU:0, one launch (start us, length us, event | category | flops | bytes accessed | tf_op | source)
XLA Modules:
  0.0 68.8 jit_solution(6472477452122624966)
XLA Ops:
  0.0 67.0 %layer.1 = bf16[64,3072]{1,0:T(8,128)(2,1)} custom-call(bf16[64,3072]{1,0:T(8,128)(2,1)} %x_ref.1, bf16[24,128]{1,0:T(8,128)(2,1)} %bitcast.4, bf16[24,128]{1,0:T(8,128)(2,1)} %bitcast.5, f32[1,128]{1,0:T(1,128)} %constant.4.clone.cos_ref, f32[1,128]{1,0:T(1,128)} %constant.5.clone.sin_ref, bf16[3072,384]{1,0:T(8,128)(2,1)} %wq_hbm.1, ...), custom_call_target="tpu_custom_call" | custom-call | tf_op jit(solution)/shard_map/layer/pallas_call | solution.py:276
  67.0 1.8 %copy.14 = bf16[64,3072]{1,0:T(8,128)(2,1)} copy(bf16[64,3072]{1,0:T(8,128)(2,1)} %layer.1) | data formatting | bytes 786432

commit v3 on v2

v3 whole, which is shorter than its diff:
```python
import math

import jax
import jax.numpy as jnp
import numpy as np
from jax import lax
from jax.experimental import pallas as pl
from jax.experimental.pallas import tpu as pltpu
from jax.sharding import PartitionSpec as P

HEAD = 128
THETA = 10000
D = 3072
B = 64
U = 4096
Q = 4
G = B // Q
NS = 3
UC = 512
ULAST = 1024
N = 8
W = D // N
HID = 1024
PARTS = ((0, 8, 9), (8, 4, 13), (12, 4, None))
GROUPS = ((0, 48), (48, 16))
QUERIES = 3
F32, BF16 = jnp.float32, jnp.bfloat16
MESH = pl.DeviceIdType.MESH


def rotary_tables():
    half = HEAD // 2
    angle = (U - 1) * THETA ** (-np.arange(half, dtype=np.float64) / half)
    cos, sin = np.cos(angle), np.sin(angle)
    return np.stack([np.concatenate([cos, cos]), np.concatenate([-sin, sin])]).astype(np.float32)


def row(gain):
    return jnp.concatenate([gain[i : i + 1] for i in range(gain.shape[0])], axis=1)


def dot(a, b):
    return jnp.dot(a, b, preferred_element_type=F32)


def layer(x_hbm, ga_hbm, gm_hbm, turn_hbm, wq_hbm, wo_hbm, wg_hbm, wu_hbm, wd_hbm, k_hbm, v_hbm, out_ref,
          x_ref, ga_ref, gm_ref, turn_ref, kbuf, vbuf, wq, wo, wg, wu, wd, qblk, sbuf, wbuf, oall, bbuf, hid, own, part1, part2, recv1, recv2, hbuf, ybuf,
          ksem, vsem, lastsem, wsem, send_sem, recv_sem):
    me = lax.axis_index("tp")
    mx, my, mc = me // 4, lax.rem(me // 2, 2), lax.rem(me, 2)

    def chip(k):
        return 2 * lax.rem(mx + k // 2, 2) + lax.rem(my + k % 2, 2)

    def at(s):
        return 2 * chip(s // 2) + lax.rem(mc + s % 2, 2)

    def kcopy(g, slot):
        return pltpu.make_async_copy(k_hbm.at[pl.ds(g * Q, Q)], kbuf.at[slot], ksem.at[slot])

    def vcopy(g, slot):
        return pltpu.make_async_copy(v_hbm.at[pl.ds(g * Q, Q)], vbuf.at[slot], vsem.at[slot])

    half = HID // 2
    loads = {"wq": pltpu.make_async_copy(wq_hbm, wq, wsem.at[0]), "wo": pltpu.make_async_copy(wo_hbm, wo, wsem.at[1])}
    for n in range(2):
        cols = pl.ds(n * half, half)
        loads["wg", n] = pltpu.make_async_copy(wg_hbm.at[:, cols], wg.at[:, cols], wsem.at[2 + n])
        loads["wu", n] = pltpu.make_async_copy(wu_hbm.at[:, cols], wu.at[:, cols], wsem.at[4 + n])
    loads["wd"] = pltpu.make_async_copy(wd_hbm, wd, wsem.at[6])
    for n, (src, dst) in enumerate(((x_hbm, x_ref), (ga_hbm, ga_ref), (gm_hbm, gm_ref), (turn_hbm, turn_ref))):
        loads["small", n] = pltpu.make_async_copy(src, dst, wsem.at[7 + n])
    last = []
    for n in range(U // ULAST):
        places = pl.ds(n * ULAST, ULAST)
        last.append(pltpu.make_async_copy(v_hbm.at[pl.ds(B - Q, Q), places], vbuf.at[(G - 1) % NS, :, places], lastsem.at[n]))

    def scatter(c, stage, rows, src, dst, s):
        return pltpu.make_async_remote_copy(src.at[at(s), rows], dst.at[s, rows], send_sem.at[stage], recv_sem.at[c, stage],
                                            device_id={"tp": at(s)}, device_id_type=MESH)

    def gather(c, stage, rows, buf, s):
        return pltpu.make_async_remote_copy(buf.at[me, rows], buf.at[me, rows], send_sem.at[stage], recv_sem.at[c, stage],
                                            device_id={"tp": at(s)}, device_id_type=MESH)

    def all_seven(c, stage, rows, buf):
        seven = buf.at[pl.ds(1, N - 1), rows]
        return pltpu.make_async_remote_copy(seven, seven, send_sem.at[stage], recv_sem.at[c, stage],
                                            device_id={"tp": at(1)}, device_id_type=MESH)

    others = (6, 7, 4, 5, 2, 3, 1)

    def part_rows(c):
        return pl.ds(PARTS[c][0] * Q, PARTS[c][1] * Q)

    def group_rows(c):
        return pl.ds(*GROUPS[c])

    with jax.named_scope("head"):
        for n in range(4):
            loads["small", n].start()
        loads["wq"].start()
        kcopy(0, 0).start()
        barrier = pltpu.get_barrier_semaphore()
        for s in range(1, N):
            pl.semaphore_signal(barrier, inc=1, device_id={"tp": at(s)}, device_id_type=MESH)
        for n in range(4):
            loads["small", n].wait()
        wide = x_ref[...].astype(F32)
        scale = lax.rsqrt(jnp.mean(wide * wide, -1, keepdims=True) + 1e-6)
        a = (wide * scale * row(ga_ref[...].astype(F32))).astype(BF16)
        loads["wq"].wait()
        kcopy(1, 1).start()
        kcopy(2, 2).start()
        vcopy(0, 0).start()
        vcopy(1, 1).start()
        loads["wo"].start()
        q = dot(a, wq[...]).astype(BF16).astype(F32)

    def picks(shape, row_axis, first):
        r = lax.broadcasted_iota(jnp.int32, shape, row_axis)
        s = lax.broadcasted_iota(jnp.int32, shape, 1 - row_axis) + first * Q
        rr = r % 16
        gg = r // 16 + first
        return [((s == gg * Q + rr - h * Q) & (rr >= h * Q) & (rr < (h + 1) * Q)).astype(BF16) for h in range(QUERIES)]

    with jax.named_scope("queries"):
        qa = jnp.zeros((16 * G, HEAD), F32)
        for h, pick in enumerate(picks((16 * G, B), 0, 0)):
            qh = q[:, h * HEAD : (h + 1) * HEAD]
            qa += dot(pick, (qh * turn_ref[0:1] + pltpu.roll(qh, HEAD // 2, 1) * turn_ref[1:2]).astype(BF16))
        block = lax.broadcasted_iota(jnp.int32, (16 * G, HEAD), 0) % Q
        for i in range(Q):
            qblk[:, i * HEAD : (i + 1) * HEAD] = jnp.where(block == i, qa, 0.0).astype(BF16)
    block = lax.broadcasted_iota(jnp.int32, (16, HEAD), 0) % Q

    def quad_rows(g):
        return pl.ds(pl.multiple_of(g * 16, 16), 16)

    def scores(g, slot, to):
        ql = qblk[quad_rows(g), :]
        for u in range(0, U, UC):
            kc = jnp.concatenate([kbuf[slot, i, u : u + UC, :] for i in range(Q)], axis=1)
            sbuf[to, :, u : u + UC] = lax.dot_general(ql, kc, (((1,), (1,)), ((), ())), preferred_element_type=F32)

    def softmax(of):
        s = sbuf[of]
        p = jnp.exp2((s - jnp.max(s, axis=1, keepdims=True)) * (HEAD**-0.5 * math.log2(math.e)))
        return (p * (1.0 / jnp.sum(p, axis=1, keepdims=True))).astype(BF16)

    def values(slot, w, first, places):
        o = jnp.zeros((16, Q * HEAD), F32)
        for u in range(first, first + places, UC):
            o += dot(w[:, u : u + UC], jnp.concatenate([vbuf[slot, i, u : u + UC, :] for i in range(Q)], axis=1))
        return o

    def keep(g, o):
        t = jnp.zeros((16, HEAD), F32)
        for i in range(Q):
            t = jnp.where(block == i, o[:, i * HEAD : (i + 1) * HEAD], t)
        oall[quad_rows(g), :] = t.astype(BF16)

    def terms(c, stage, rows, a, w_ref, part, recv):
        for n in range(4):
            t = dot(a, w_ref[:, n * 2 * W : (n + 1) * 2 * W])
            for j in range(2):
                own[2 * n + j, rows] = t[:, j * W : (j + 1) * W]
                part[2 * n + j, rows] = t[:, j * W : (j + 1) * W].astype(BF16)
        for s in others:
            scatter(c, stage, rows, part, recv, s).start()

    def finish(c):
        first, quads, _ = PARTS[c]
        o = oall[first * 16 : (first + quads) * 16, :]
        seen = [dot(pick, o).astype(BF16) for pick in picks((quads * Q, quads * 16), 1, first)]
        if c == 0:
            loads["wo"].wait()
            pl.semaphore_wait(barrier, N - 1)
        terms(c, 0, part_rows(c), jnp.concatenate(seen, axis=1), wo, part1, recv1)

    def summed(c, stage, rows, part, recv):
        all_seven(c, stage, rows, recv).wait_recv()
        t = own[me, rows]
        for s in range(1, N):
            t += recv[s, rows].astype(F32)
        return t

    def reduce1(c):
        rows = part_rows(c)
        mine = x_ref[rows, pl.ds(pl.multiple_of(me * W, 128), W)].astype(F32)
        hbuf[me, rows] = (mine + summed(c, 0, rows, part1, recv1)).astype(BF16)
        for s in others:
            gather(c, 1, rows, hbuf, s).start()

    def reduce2(c):
        rows = group_rows(c)
        ybuf[me, rows] = (hbuf[me, rows].astype(F32) + summed(c, 2, rows, part2, recv2)).astype(BF16)
        for s in others:
            gather(c, 3, rows, ybuf, s).start()

    def norm2(c, parts):
        for p in parts:
            all_seven(p, 1, part_rows(p), hbuf).wait_recv()
        rows = group_rows(c)
        squares = jnp.zeros((GROUPS[c][1], 1), F32)
        for j in range(N):
            t = hbuf[j, rows].astype(F32)
            squares += jnp.sum(t * t, -1, keepdims=True)
        scale = lax.rsqrt(squares * (1.0 / D) + 1e-6)
        gain = row(gm_ref[...].astype(F32))
        for j in range(N):
            bbuf[rows, j * W : (j + 1) * W] = (hbuf[j, rows].astype(F32) * scale * gain[:, j * W : (j + 1) * W]).astype(BF16)

    def hidden(c, n):
        rows = group_rows(c)
        if c == 0:
            loads["wg", n].wait()
            loads["wu", n].wait()
        b = bbuf[rows, :]
        gate = dot(b, wg[:, n * half : (n + 1) * half])
        up = dot(b, wu[:, n * half : (n + 1) * half])
        hid[rows, n * half : (n + 1) * half] = (jax.nn.silu(gate) * up).astype(BF16)

    def down(c):
        rows = group_rows(c)
        if c == 0:
            loads["wd"].wait()
        terms(c, 2, rows, hid[rows, :], wd, part2, recv2)

    with jax.named_scope("k0wait"):
        kcopy(0, 0).wait()
    scores(0, 0, 0)
    kcopy(3, 0).start()
    with jax.named_scope("k1wait"):
        kcopy(1, 1).wait()
    wbuf[0] = softmax(0)
    scores(1, 1, 1)

    def body(g, _):
        kslot, vslot = lax.rem(g + 2, NS), lax.rem(g, NS)
        with jax.named_scope("loopwait"):
            kcopy(g + 2, kslot).wait()
            vcopy(g, vslot).wait()

        @pl.when(g + 4 < G)
        def _():
            kcopy(g + 4, lax.rem(g + 4, NS)).start()

        @pl.when(g + 2 < G - 1)
        def _():
            vcopy(g + 2, lax.rem(g + 2, NS)).start()

        @pl.when(g + 2 == G - 1)
        def _():
            for copy in last:
                copy.start()
            for n in range(2):
                loads["wg", n].start(priority=1)
                loads["wu", n].start(priority=1)
            loads["wd"].start(priority=1)

        keep(g, values(vslot, wbuf.at[lax.rem(g, 2)], 0, U))
        wbuf[lax.rem(g + 1, 2)] = softmax(lax.rem(g + 1, NS))
        scores(g + 2, kslot, kslot)

        for c, (first, quads, reduced) in enumerate(PARTS[:-1]):
            @pl.when(g == first + quads - 1)
            def _(c=c):
                with jax.named_scope(f"finish{c}"):
                    finish(c)

            if reduced is not None:
                @pl.when(g == reduced)
                def _(c=c):
                    with jax.named_scope(f"reduce1_{c}"):
                        reduce1(c)

        return 0

    with jax.named_scope("loop"):
        lax.fori_loop(0, G - 2, body, 0)
    with jax.named_scope("v14"):
        vcopy(G - 2, (G - 2) % NS).wait()
    keep(G - 2, values((G - 2) % NS, wbuf.at[(G - 2) % 2], 0, U))
    wbuf[(G - 1) % 2] = softmax((G - 1) % NS)
    o = jnp.zeros((16, Q * HEAD), F32)
    for n, copy in enumerate(last):
        with jax.named_scope(f"last{n}"):
            copy.wait()
        o += values((G - 1) % NS, wbuf.at[(G - 1) % 2], n * ULAST, ULAST)
    keep(G - 1, o)
    with jax.named_scope("f2"):
        finish(2)
    with jax.named_scope("n0"):
        norm2(0, (0, 1))
    with jax.named_scope("h00"):
        hidden(0, 0)
    with jax.named_scope("r12"):
        reduce1(2)
    with jax.named_scope("h01"):
        hidden(0, 1)
    with jax.named_scope("d0"):
        down(0)
    with jax.named_scope("n1"):
        norm2(1, (2,))
    with jax.named_scope("h10"):
        hidden(1, 0)
    with jax.named_scope("h11"):
        hidden(1, 1)
    with jax.named_scope("d1"):
        down(1)
    with jax.named_scope("r20"):
        reduce2(0)
    with jax.named_scope("r21"):
        reduce2(1)
    for c in range(len(GROUPS)):
        rows = group_rows(c)
        with jax.named_scope(f"out{c}"):
            all_seven(c, 3, rows, ybuf).wait_recv()
        for j in range(N):
            out_ref[rows, j * W : (j + 1) * W] = ybuf[j, rows]
    with jax.named_scope("sent"):
        for stage, buf in enumerate((part1, hbuf, part2, ybuf)):
            all_seven(0, stage, pl.ds(0, B), buf).wait_send()


def solution(mesh):
    any_, vmem = pl.BlockSpec(memory_space=pl.ANY), pl.BlockSpec(memory_space=pltpu.VMEM)

    def step(x, k_cache, v_cache, gain_a, wq, wo, gain_m, w_gate, w_up, w_down):
        return pl.pallas_call(
            layer,
            out_shape=pltpu.VMEM((B, D), BF16),
            in_specs=[any_] * 11,
            out_specs=vmem,
            scratch_shapes=[
                pltpu.VMEM((B, D), BF16),
                pltpu.VMEM((D // 128, 128), BF16),
                pltpu.VMEM((D // 128, 128), BF16),
                pltpu.VMEM((2, HEAD), F32),
                pltpu.VMEM((NS, Q, U, HEAD), BF16),
                pltpu.VMEM((NS, Q, U, HEAD), BF16),
                pltpu.VMEM((D, QUERIES * HEAD), BF16),
                pltpu.VMEM((QUERIES * HEAD, D), BF16),
                pltpu.VMEM((D, HID), BF16),
                pltpu.VMEM((D, HID), BF16),
                pltpu.VMEM((HID, D), BF16),
                pltpu.VMEM((16 * G, Q * HEAD), BF16),
                pltpu.VMEM((NS, 16, U), F32),
                pltpu.VMEM((2, 16, U), BF16),
                pltpu.VMEM((16 * G, HEAD), BF16),
                pltpu.VMEM((B, D), BF16),
                pltpu.VMEM((B, HID), BF16),
                pltpu.VMEM((N, B, W), F32),
                *[pltpu.VMEM((N, B, W), BF16)] * 6,
                pltpu.SemaphoreType.DMA((NS,)),
                pltpu.SemaphoreType.DMA((NS,)),
                pltpu.SemaphoreType.DMA((U // ULAST,)),
                pltpu.SemaphoreType.DMA((11,)),
                pltpu.SemaphoreType.DMA((4,)),
                pltpu.SemaphoreType.DMA((len(PARTS), 4)),
            ],
            compiler_params=pltpu.CompilerParams(collective_id=0, has_side_effects=True, vmem_limit_bytes=56 * 2**20),
            name="layer",
        )(x, gain_a.reshape(-1, 128), gain_m.reshape(-1, 128), jnp.asarray(rotary_tables()), wq, wo, w_gate, w_up, w_down,
          k_cache.reshape(B, U, HEAD), v_cache.reshape(B, U, HEAD))

    states, cache, columns, rows_of = P("dp", None), P("dp", None, "tp", None), P(None, "tp"), P("tp", None)
    return jax.shard_map(
        step,
        mesh=mesh,
        in_specs=(states, cache, cache, P(None), columns, rows_of, P(None), columns, columns, rows_of),
        out_specs=states,
        check_vma=False,
    )
```

time: 68.9 us -> 63.2 us (0.917)
  Pallas kernels: 67 us -> 62.3 us
  local copies, waits for them, and re-layouts: 1.77 us -> 0.75 us
    pallas_call x1, Pallas kernels: 67 us -> 62.3 us  [step(): pl.pallas_call(layer, out_shape=pltpu.VMEM((B, D), BF16), in_specs=[any_]...]
    unnamed x1, local copies, waits for them, and re-layouts: 1.77 us -> 0.75 us
where the time goes in v3:
time: 63.2 us; the launch traced here: 63.1 us
  Pallas kernels  62.3 us (99%)
  local copies, waits for them, and re-layouts  0.75 us (1%)
    pallas_call x1, Pallas kernels, step(): pl.pallas_call(layer, out_shape=pltpu.VMEM((B, D), BF16), in_specs=[any_]...  62.3 us

profile of v3, /device:TPU:0, one launch (start us, length us, event | category | flops | bytes accessed | tf_op | source)
XLA Modules:
  0.0 63.1 jit_solution(8585123138891328339)
XLA Ops:
  0.0 62.3 %layer.1 = bf16[64,3072]{1,0:T(8,128)(2,1)S(1)} custom-call(bf16[64,3072]{1,0:T(8,128)(2,1)} %x_hbm.1, bf16[24,128]{1,0:T(8,128)(2,1)} %bitcast.4, bf16[24,128]{1,0:T(8,128)(2,1)} %bitcast.5, f32[2,128]{1,0:T(2,128)} %constant.2.clone.turn_hbm, bf16[3072,384]{1,0:T(8,128)(2,1)} %wq_hbm.1, bf16[384,3072]{1,0:T(8,128)(2,1)} %wo_hbm.1, ...), custom_call_target="tpu_custom_call" | custom-call | tf_op jit(solution)/shard_map/layer/pallas_call | solution.py:331
  62.3 0.7 %copy.13 = bf16[64,3072]{1,0:T(8,128)(2,1)} copy(bf16[64,3072]{1,0:T(8,128)(2,1)S(1)} %layer.1) | data formatting | bytes 786432

commit v4 on v3

--- a/solution.py
+++ b/solution.py
@@ -16,14 +16,17 @@
 Q = 4
 G = B // Q
 NS = 3
+VS = 4
+LEAD = 3
 UC = 512
 ULAST = 1024
 N = 8
 W = D // N
 HID = 1024
-PARTS = ((0, 8, 9), (8, 4, 13), (12, 4, None))
+PARTS = ((0, 8, 9), (8, 4, None), (12, 4, None))
 GROUPS = ((0, 48), (48, 16))
 QUERIES = 3
+FAR_FIRST = ((3, 2), (1, 0))
 F32, BF16 = jnp.float32, jnp.bfloat16
 MESH = pl.DeviceIdType.MESH
 
@@ -55,6 +58,9 @@
     def at(s):
         return 2 * chip(s // 2) + lax.rem(mc + s % 2, 2)
 
+    def chip_columns(k):
+        return pl.ds(pl.multiple_of(chip(k) * (2 * W), 128), 2 * W)
+
     def kcopy(g, slot):
         return pltpu.make_async_copy(k_hbm.at[pl.ds(g * Q, Q)], kbuf.at[slot], ksem.at[slot])
 
@@ -62,18 +68,26 @@
         return pltpu.make_async_copy(v_hbm.at[pl.ds(g * Q, Q)], vbuf.at[slot], vsem.at[slot])
 
     half = HID // 2
-    loads = {"wq": pltpu.make_async_copy(wq_hbm, wq, wsem.at[0]), "wo": pltpu.make_async_copy(wo_hbm, wo, wsem.at[1])}
+    loads = {"wq": pltpu.make_async_copy(wq_hbm, wq, wsem.at[4]), "wo": pltpu.make_async_copy(wo_hbm, wo, wsem.at[3])}
     for n in range(2):
         cols = pl.ds(n * half, half)
-        loads["wg", n] = pltpu.make_async_copy(wg_hbm.at[:, cols], wg.at[:, cols], wsem.at[2 + n])
-        loads["wu", n] = pltpu.make_async_copy(wu_hbm.at[:, cols], wu.at[:, cols], wsem.at[4 + n])
-    loads["wd"] = pltpu.make_async_copy(wd_hbm, wd, wsem.at[6])
+        loads["wg", n] = pltpu.make_async_copy(wg_hbm.at[:, cols], wg.at[:, cols], wsem.at[n])
+        loads["wu", n] = pltpu.make_async_copy(wu_hbm.at[:, cols], wu.at[:, cols], wsem.at[n])
+    for h, ks in enumerate(FAR_FIRST):
+        for k in ks:
+            cols = chip_columns(k)
+            loads["wd", k] = pltpu.make_async_copy(wd_hbm.at[:, cols], wd.at[:, cols], wsem.at[2 + h])
+    down_halves = [pltpu.make_async_copy(wd_hbm.at[:, pl.ds(0, D // 2)], wd.at[:, pl.ds(0, D // 2)], wsem.at[2 + h]) for h in range(2)]
     for n, (src, dst) in enumerate(((x_hbm, x_ref), (ga_hbm, ga_ref), (gm_hbm, gm_ref), (turn_hbm, turn_ref))):
-        loads["small", n] = pltpu.make_async_copy(src, dst, wsem.at[7 + n])
+        loads["small", n] = pltpu.make_async_copy(src, dst, wsem.at[n])
+
+    def both_halves(n):
+        return pltpu.make_async_copy(wg_hbm, wg, wsem.at[n])
+
     last = []
     for n in range(U // ULAST):
         places = pl.ds(n * ULAST, ULAST)
-        last.append(pltpu.make_async_copy(v_hbm.at[pl.ds(B - Q, Q), places], vbuf.at[(G - 1) % NS, :, places], lastsem.at[n]))
+        last.append(pltpu.make_async_copy(v_hbm.at[pl.ds(B - Q, Q), places], vbuf.at[(G - 1) % VS, :, places], lastsem.at[n]))
 
     def scatter(c, stage, rows, src, dst, s):
         return pltpu.make_async_remote_copy(src.at[at(s), rows], dst.at[s, rows], send_sem.at[stage], recv_sem.at[c, stage],
@@ -160,14 +174,18 @@
             t = jnp.where(block == i, o[:, i * HEAD : (i + 1) * HEAD], t)
         oall[quad_rows(g), :] = t.astype(BF16)
 
-    def terms(c, stage, rows, a, w_ref, part, recv):
-        for n in range(4):
-            t = dot(a, w_ref[:, n * 2 * W : (n + 1) * 2 * W])
-            for j in range(2):
-                own[2 * n + j, rows] = t[:, j * W : (j + 1) * W]
-                part[2 * n + j, rows] = t[:, j * W : (j + 1) * W].astype(BF16)
-        for s in others:
-            scatter(c, stage, rows, part, recv, s).start()
+    def terms(c, stage, rows, a, w_ref, part, recv, ready=None):
+        for h, ks in enumerate(FAR_FIRST):
+            if ready is not None:
+                ready[h].wait()
+            for k in ks:
+                t = dot(a, w_ref[:, chip_columns(k)])
+                for j in range(2):
+                    own[2 * chip(k) + j, rows] = t[:, j * W : (j + 1) * W]
+                    part[2 * chip(k) + j, rows] = t[:, j * W : (j + 1) * W].astype(BF16)
+            for s in [2 * k + j for k in ks for j in range(2)]:
+                if s:
+                    scatter(c, stage, rows, part, recv, s).start()
 
     def finish(c):
         first, quads, _ = PARTS[c]
@@ -195,14 +213,27 @@
     def reduce2(c):
         rows = group_rows(c)
         ybuf[me, rows] = (hbuf[me, rows].astype(F32) + summed(c, 2, rows, part2, recv2)).astype(BF16)
-        for s in others:
-            gather(c, 3, rows, ybuf, s).start()
-
-    def norm2(c, parts):
-        for p in parts:
-            all_seven(p, 1, part_rows(p), hbuf).wait_recv()
-        rows = group_rows(c)
-        squares = jnp.zeros((GROUPS[c][1], 1), F32)
+        if c == 0:
+            for k in (3, 2, 1):
+                gather(0, 3, rows, ybuf, 2 * k).start()
+            across(0).start()
+        else:
+            for s in others:
+                gather(c, 3, rows, ybuf, s).start()
+
+    def across(k):
+        block = ybuf.at[2 * chip(k) + mc, group_rows(0)]
+        return pltpu.make_async_remote_copy(block, block, send_sem.at[3], recv_sem.at[2, 3], device_id={"tp": at(1)}, device_id_type=MESH)
+
+    def some(n, c, stage, rows, buf):
+        blocks = buf.at[pl.ds(0, n), rows]
+        return pltpu.make_async_remote_copy(blocks, blocks, send_sem.at[stage], recv_sem.at[c, stage],
+                                            device_id={"tp": at(1)}, device_id_type=MESH)
+
+    def norm2(c):
+        rows = part_rows(c)
+        all_seven(c, 1, rows, hbuf).wait_recv()
+        squares = jnp.zeros((PARTS[c][1] * Q, 1), F32)
         for j in range(N):
             t = hbuf[j, rows].astype(F32)
             squares += jnp.sum(t * t, -1, keepdims=True)
@@ -211,57 +242,50 @@
         for j in range(N):
             bbuf[rows, j * W : (j + 1) * W] = (hbuf[j, rows].astype(F32) * scale * gain[:, j * W : (j + 1) * W]).astype(BF16)
 
-    def hidden(c, n):
-        rows = group_rows(c)
-        if c == 0:
-            loads["wg", n].wait()
-            loads["wu", n].wait()
+    def hidden(c, first, width):
+        rows, cols = group_rows(c), pl.ds(first, width)
         b = bbuf[rows, :]
-        gate = dot(b, wg[:, n * half : (n + 1) * half])
-        up = dot(b, wu[:, n * half : (n + 1) * half])
-        hid[rows, n * half : (n + 1) * half] = (jax.nn.silu(gate) * up).astype(BF16)
+        hid[rows, cols] = (jax.nn.silu(dot(b, wg[:, cols])) * dot(b, wu[:, cols])).astype(BF16)
 
     def down(c):
         rows = group_rows(c)
-        if c == 0:
-            loads["wd"].wait()
-        terms(c, 2, rows, hid[rows, :], wd, part2, recv2)
+        terms(c, 2, rows, hid[rows, :], wd, part2, recv2, down_halves if c == 0 else None)
 
     with jax.named_scope("k0wait"):
         kcopy(0, 0).wait()
     scores(0, 0, 0)
     kcopy(3, 0).start()
+    wbuf[0] = softmax(0)
     with jax.named_scope("k1wait"):
         kcopy(1, 1).wait()
-    wbuf[0] = softmax(0)
     scores(1, 1, 1)
+    kcopy(4, 1).start()
+    with jax.named_scope("k2wait"):
+        kcopy(2, 2).wait()
+    scores(2, 2, 2)
+
+    def attended(g):
+        keep(g, values(lax.rem(g, VS), wbuf.at[lax.rem(g, 2)], 0, U))
+        wbuf[lax.rem(g + 1, 2)] = softmax(lax.rem(g + 1, LEAD + 1))
 
     def body(g, _):
-        kslot, vslot = lax.rem(g + 2, NS), lax.rem(g, NS)
+        @pl.when(g + LEAD + 2 < G)
+        def _():
+            kcopy(g + LEAD + 2, lax.rem(g + LEAD + 2, NS)).start()
+
+        vcopy(g + 2, lax.rem(g + 2, VS)).start()
+        kslot = lax.rem(g + LEAD, NS)
         with jax.named_scope("loopwait"):
-            kcopy(g + 2, kslot).wait()
-            vcopy(g, vslot).wait()
-
-        @pl.when(g + 4 < G)
-        def _():
-            kcopy(g + 4, lax.rem(g + 4, NS)).start()
-
-        @pl.when(g + 2 < G - 1)
-        def _():
-            vcopy(g + 2, lax.rem(g + 2, NS)).start()
-
-        @pl.when(g + 2 == G - 1)
+            kcopy(g + LEAD, kslot).wait()
+            vcopy(g, lax.rem(g, VS)).wait()
+
+        @pl.when(g == G - LEAD - 1)
         def _():
             for copy in last:
                 copy.start()
-            for n in range(2):
-                loads["wg", n].start(priority=1)
-                loads["wu", n].start(priority=1)
-            loads["wd"].start(priority=1)
-
-        keep(g, values(vslot, wbuf.at[lax.rem(g, 2)], 0, U))
-        wbuf[lax.rem(g + 1, 2)] = softmax(lax.rem(g + 1, NS))
-        scores(g + 2, kslot, kslot)
+
+        attended(g)
+        scores(g + LEAD, kslot, lax.rem(g + LEAD, LEAD + 1))
 
         for c, (first, quads, reduced) in enumerate(PARTS[:-1]):
             @pl.when(g == first + quads - 1)
@@ -278,47 +302,67 @@
         return 0
 
     with jax.named_scope("loop"):
-        lax.fori_loop(0, G - 2, body, 0)
-    with jax.named_scope("v14"):
-        vcopy(G - 2, (G - 2) % NS).wait()
-    keep(G - 2, values((G - 2) % NS, wbuf.at[(G - 2) % 2], 0, U))
-    wbuf[(G - 1) % 2] = softmax((G - 1) % NS)
+        lax.fori_loop(0, G - LEAD, body, 0)
+    for g in range(G - LEAD, G - 1):
+        with jax.named_scope(f"v{g}"):
+            vcopy(g, g % VS).wait()
+        attended(g)
+    for n in range(2):
+        loads["wg", n].start()
+        loads["wu", n].start()
+    for ks in FAR_FIRST:
+        for k in ks:
+            loads["wd", k].start()
+    with jax.named_scope("r11"):
+        reduce1(1)
     o = jnp.zeros((16, Q * HEAD), F32)
     for n, copy in enumerate(last):
         with jax.named_scope(f"last{n}"):
             copy.wait()
-        o += values((G - 1) % NS, wbuf.at[(G - 1) % 2], n * ULAST, ULAST)
+        o += values((G - 1) % VS, wbuf.at[(G - 1) % 2], n * ULAST, ULAST)
     keep(G - 1, o)
     with jax.named_scope("f2"):
         finish(2)
     with jax.named_scope("n0"):
-        norm2(0, (0, 1))
+        norm2(0)
+    with jax.named_scope("n01"):
+        norm2(1)
     with jax.named_scope("h00"):
-        hidden(0, 0)
+        both_halves(0).wait()
+        hidden(0, 0 * half, half)
     with jax.named_scope("r12"):
         reduce1(2)
     with jax.named_scope("h01"):
-        hidden(0, 1)
+        both_halves(1).wait()
+        hidden(0, 1 * half, half)
     with jax.named_scope("d0"):
         down(0)
     with jax.named_scope("n1"):
-        norm2(1, (2,))
-    with jax.named_scope("h10"):
-        hidden(1, 0)
-    with jax.named_scope("h11"):
-        hidden(1, 1)
+        norm2(2)
+    with jax.named_scope("h1"):
+        hidden(1, 0, HID)
     with jax.named_scope("d1"):
         down(1)
     with jax.named_scope("r20"):
         reduce2(0)
     with jax.named_scope("r21"):
         reduce2(1)
-    for c in range(len(GROUPS)):
+    with jax.named_scope("across"):
+        some(N // 2 - 1, 0, 3, group_rows(0), ybuf).wait_recv()
+        for k in (3, 2, 1):
+            across(k).start()
+
+    def put(c):
         rows = group_rows(c)
-        with jax.named_scope(f"out{c}"):
-            all_seven(c, 3, rows, ybuf).wait_recv()
         for j in range(N):
             out_ref[rows, j * W : (j + 1) * W] = ybuf[j, rows]
+
+    with jax.named_scope("out0"):
+        some(N // 2, 2, 3, group_rows(0), ybuf).wait_recv()
+    put(0)
+    with jax.named_scope("out1"):
+        all_seven(1, 3, group_rows(1), ybuf).wait_recv()
+    put(1)
     with jax.named_scope("sent"):
         for stage, buf in enumerate((part1, hbuf, part2, ybuf)):
             all_seven(0, stage, pl.ds(0, B), buf).wait_send()
@@ -339,14 +383,14 @@
                 pltpu.VMEM((D // 128, 128), BF16),
                 pltpu.VMEM((2, HEAD), F32),
                 pltpu.VMEM((NS, Q, U, HEAD), BF16),
-                pltpu.VMEM((NS, Q, U, HEAD), BF16),
+                pltpu.VMEM((VS, Q, U, HEAD), BF16),
                 pltpu.VMEM((D, QUERIES * HEAD), BF16),
                 pltpu.VMEM((QUERIES * HEAD, D), BF16),
                 pltpu.VMEM((D, HID), BF16),
                 pltpu.VMEM((D, HID), BF16),
                 pltpu.VMEM((HID, D), BF16),
                 pltpu.VMEM((16 * G, Q * HEAD), BF16),
-                pltpu.VMEM((NS, 16, U), F32),
+                pltpu.VMEM((LEAD + 1, 16, U), F32),
                 pltpu.VMEM((2, 16, U), BF16),
                 pltpu.VMEM((16 * G, HEAD), BF16),
                 pltpu.VMEM((B, D), BF16),
@@ -354,13 +398,13 @@
                 pltpu.VMEM((N, B, W), F32),
                 *[pltpu.VMEM((N, B, W), BF16)] * 6,
                 pltpu.SemaphoreType.DMA((NS,)),
-                pltpu.SemaphoreType.DMA((NS,)),
+                pltpu.SemaphoreType.DMA((VS,)),
                 pltpu.SemaphoreType.DMA((U // ULAST,)),
-                pltpu.SemaphoreType.DMA((11,)),
+                pltpu.SemaphoreType.DMA((5,)),
                 pltpu.SemaphoreType.DMA((4,)),
                 pltpu.SemaphoreType.DMA((len(PARTS), 4)),
             ],
-            compiler_params=pltpu.CompilerParams(collective_id=0, has_side_effects=True, vmem_limit_bytes=56 * 2**20),
+            compiler_params=pltpu.CompilerParams(collective_id=0, has_side_effects=True, vmem_limit_bytes=60 * 2**20),
             name="layer",
         )(x, gain_a.reshape(-1, 128), gain_m.reshape(-1, 128), jnp.asarray(rotary_tables()), wq, wo, w_gate, w_up, w_down,
           k_cache.reshape(B, U, HEAD), v_cache.reshape(B, U, HEAD))

time: 63.2 us -> 61.6 us (0.975)
  Pallas kernels: 62.3 us -> 60.7 us
    pallas_call x1, Pallas kernels: 62.3 us -> 60.7 us  [step(): pl.pallas_call(layer, out_shape=pltpu.VMEM((B, D), BF16), in_specs=[any_]...]
where the time goes in v4:
time: 61.6 us; the launch traced here: 61.5 us
  Pallas kernels  60.7 us (99%)
  local copies, waits for them, and re-layouts  0.75 us (1%)
    pallas_call x1, Pallas kernels, step(): pl.pallas_call(layer, out_shape=pltpu.VMEM((B, D), BF16), in_specs=[any_]...  60.7 us

profile of v4, /device:TPU:0, one launch (start us, length us, event | category | flops | bytes accessed | tf_op | source)
XLA Modules:
  0.0 61.5 jit_solution(1549132356135664656)
XLA Ops:
  0.0 60.7 %layer.1 = bf16[64,3072]{1,0:T(8,128)(2,1)S(1)} custom-call(bf16[64,3072]{1,0:T(8,128)(2,1)} %x_hbm.1, bf16[24,128]{1,0:T(8,128)(2,1)} %bitcast.4, bf16[24,128]{1,0:T(8,128)(2,1)} %bitcast.5, f32[2,128]{1,0:T(2,128)} %constant.2.clone.turn_hbm, bf16[3072,384]{1,0:T(8,128)(2,1)} %wq_hbm.1, bf16[384,3072]{1,0:T(8,128)(2,1)} %wo_hbm.1, ...), custom_call_target="tpu_custom_call" | custom-call | tf_op jit(solution)/shard_map/layer/pallas_call | solution.py:375
  60.7 0.7 %copy.13 = bf16[64,3072]{1,0:T(8,128)(2,1)} copy(bf16[64,3072]{1,0:T(8,128)(2,1)S(1)} %layer.1) | data formatting | bytes 786432

commit v5 on v4

--- a/solution.py
+++ b/solution.py
@@ -23,7 +23,8 @@
 N = 8
 W = D // N
 HID = 1024
-PARTS = ((0, 8, 9), (8, 4, None), (12, 4, None))
+PARTS = ((0, 8), (8, 4), (12, 4))
+REDUCE_AT = 9
 GROUPS = ((0, 48), (48, 16))
 QUERIES = 3
 FAR_FIRST = ((3, 2), (1, 0))
@@ -47,7 +48,7 @@
 
 
 def layer(x_hbm, ga_hbm, gm_hbm, turn_hbm, wq_hbm, wo_hbm, wg_hbm, wu_hbm, wd_hbm, k_hbm, v_hbm, out_ref,
-          x_ref, ga_ref, gm_ref, turn_ref, kbuf, vbuf, wq, wo, wg, wu, wd, qblk, sbuf, wbuf, oall, bbuf, hid, own, part1, part2, recv1, recv2, hbuf, ybuf,
+          x_ref, ga_ref, gm_ref, turn_ref, kbuf, vbuf, wq, wo, wg, wu, wd, qblk, sbuf, wbuf, seen, bbuf, hid, own, part1, part2, recv1, recv2, hbuf, ybuf,
           ksem, vsem, lastsem, wsem, send_sem, recv_sem):
     me = lax.axis_index("tp")
     mx, my, mc = me // 4, lax.rem(me // 2, 2), lax.rem(me, 2)
@@ -172,7 +173,8 @@
         t = jnp.zeros((16, HEAD), F32)
         for i in range(Q):
             t = jnp.where(block == i, o[:, i * HEAD : (i + 1) * HEAD], t)
-        oall[quad_rows(g), :] = t.astype(BF16)
+        for h in range(QUERIES):
+            seen[g, :, h * HEAD : (h + 1) * HEAD] = t[h * Q : (h + 1) * Q]
 
     def terms(c, stage, rows, a, w_ref, part, recv, ready=None):
         for h, ks in enumerate(FAR_FIRST):
@@ -188,13 +190,12 @@
                     scatter(c, stage, rows, part, recv, s).start()
 
     def finish(c):
-        first, quads, _ = PARTS[c]
-        o = oall[first * 16 : (first + quads) * 16, :]
-        seen = [dot(pick, o).astype(BF16) for pick in picks((quads * Q, quads * 16), 1, first)]
         if c == 0:
             loads["wo"].wait()
             pl.semaphore_wait(barrier, N - 1)
-        terms(c, 0, part_rows(c), jnp.concatenate(seen, axis=1), wo, part1, recv1)
+        first, quads = PARTS[c]
+        rows = jnp.concatenate([seen[g] for g in range(first, first + quads)], axis=0).astype(BF16)
+        terms(c, 0, part_rows(c), rows, wo, part1, recv1)
 
     def summed(c, stage, rows, part, recv):
         all_seven(c, stage, rows, recv).wait_recv()
@@ -264,57 +265,72 @@
         kcopy(2, 2).wait()
     scores(2, 2, 2)
 
+    def mod(g, n):
+        return g % n if isinstance(g, int) else lax.rem(g, n)
+
     def attended(g):
-        keep(g, values(lax.rem(g, VS), wbuf.at[lax.rem(g, 2)], 0, U))
-        wbuf[lax.rem(g + 1, 2)] = softmax(lax.rem(g + 1, LEAD + 1))
+        keep(g, values(mod(g, VS), wbuf.at[mod(g, 2)], 0, U))
+        wbuf[mod(g + 1, 2)] = softmax(mod(g + 1, LEAD + 1))
+
+    def arrive(g):
+        kcopy(g + LEAD, mod(g + LEAD, NS)).wait()
+        vcopy(g, mod(g, VS)).wait()
+
+    def ahead(g):
+        scores(g + LEAD, mod(g + LEAD, NS), mod(g + LEAD, LEAD + 1))
 
     def body(g, _):
         @pl.when(g + LEAD + 2 < G)
         def _():
-            kcopy(g + LEAD + 2, lax.rem(g + LEAD + 2, NS)).start()
-
-        vcopy(g + 2, lax.rem(g + 2, VS)).start()
-        kslot = lax.rem(g + LEAD, NS)
+            kcopy(g + LEAD + 2, mod(g + LEAD + 2, NS)).start()
+
+        vcopy(g + 2, mod(g + 2, VS)).start()
         with jax.named_scope("loopwait"):
-            kcopy(g + LEAD, kslot).wait()
-            vcopy(g, lax.rem(g, VS)).wait()
-
-        @pl.when(g == G - LEAD - 1)
+            arrive(g)
+        attended(g)
+        ahead(g)
+
+        @pl.when(g == PARTS[0][1] - 1)
         def _():
-            for copy in last:
-                copy.start()
-
-        attended(g)
-        scores(g + LEAD, kslot, lax.rem(g + LEAD, LEAD + 1))
-
-        for c, (first, quads, reduced) in enumerate(PARTS[:-1]):
-            @pl.when(g == first + quads - 1)
-            def _(c=c):
-                with jax.named_scope(f"finish{c}"):
-                    finish(c)
-
-            if reduced is not None:
-                @pl.when(g == reduced)
-                def _(c=c):
-                    with jax.named_scope(f"reduce1_{c}"):
-                        reduce1(c)
+            with jax.named_scope("finish0"):
+                finish(0)
+
+        @pl.when(g == REDUCE_AT)
+        def _():
+            with jax.named_scope("reduce1_0"):
+                reduce1(0)
 
         return 0
 
     with jax.named_scope("loop"):
-        lax.fori_loop(0, G - LEAD, body, 0)
-    for g in range(G - LEAD, G - 1):
-        with jax.named_scope(f"v{g}"):
-            vcopy(g, g % VS).wait()
-        attended(g)
+        lax.fori_loop(0, G - LEAD - 2, body, 0)
+    vcopy(G - LEAD, (G - LEAD) % VS).start()
+    arrive(G - LEAD - 2)
+    attended(G - LEAD - 2)
+    with jax.named_scope("finish1"):
+        finish(1)
+    ahead(G - LEAD - 2)
+    vcopy(G - LEAD + 1, (G - LEAD + 1) % VS).start()
+    with jax.named_scope("arrive12"):
+        arrive(G - LEAD - 1)
+    for copy in last:
+        copy.start()
+    attended(G - LEAD - 1)
+    ahead(G - LEAD - 1)
+    with jax.named_scope("v13"):
+        vcopy(G - LEAD, (G - LEAD) % VS).wait()
+    attended(G - LEAD)
+    with jax.named_scope("r11"):
+        reduce1(1)
+    with jax.named_scope("v14"):
+        vcopy(G - LEAD + 1, (G - LEAD + 1) % VS).wait()
+    attended(G - LEAD + 1)
     for n in range(2):
         loads["wg", n].start()
         loads["wu", n].start()
     for ks in FAR_FIRST:
         for k in ks:
             loads["wd", k].start()
-    with jax.named_scope("r11"):
-        reduce1(1)
     o = jnp.zeros((16, Q * HEAD), F32)
     for n, copy in enumerate(last):
         with jax.named_scope(f"last{n}"):
@@ -392,7 +408,7 @@
                 pltpu.VMEM((16 * G, Q * HEAD), BF16),
                 pltpu.VMEM((LEAD + 1, 16, U), F32),
                 pltpu.VMEM((2, 16, U), BF16),
-                pltpu.VMEM((16 * G, HEAD), BF16),
+                pltpu.VMEM((G, Q, QUERIES * HEAD), F32),
                 pltpu.VMEM((B, D), BF16),
                 pltpu.VMEM((B, HID), BF16),
                 pltpu.VMEM((N, B, W), F32),

time: 61.6 us -> 61.2 us (level)
  no operation moved by 1% of the time
where the time goes in v5:
time: 61.2 us
  Pallas kernels  60.4 us (99%)
  local copies, waits for them, and re-layouts  0.75 us (1%)
    pallas_call x1, Pallas kernels, step(): pl.pallas_call(layer, out_shape=pltpu.VMEM((B, D), BF16), in_specs=[any_]...  60.4 us

profile of v5, /device:TPU:0, one launch (start us, length us, event | category | flops | bytes accessed | tf_op | source)
XLA Modules:
  0.0 61.2 jit_solution(7305767756208775036)
XLA Ops:
  0.0 60.4 %layer.1 = bf16[64,3072]{1,0:T(8,128)(2,1)S(1)} custom-call(bf16[64,3072]{1,0:T(8,128)(2,1)} %x_hbm.1, bf16[24,128]{1,0:T(8,128)(2,1)} %bitcast.4, bf16[24,128]{1,0:T(8,128)(2,1)} %bitcast.5, f32[2,128]{1,0:T(2,128)} %constant.2.clone.turn_hbm, bf16[3072,384]{1,0:T(8,128)(2,1)} %wq_hbm.1, bf16[384,3072]{1,0:T(8,128)(2,1)} %wo_hbm.1, ...), custom_call_target="tpu_custom_call" | custom-call | tf_op jit(solution)/shard_map/layer/pallas_call | solution.py:391
  60.4 0.7 %copy.13 = bf16[64,3072]{1,0:T(8,128)(2,1)} copy(bf16[64,3072]{1,0:T(8,128)(2,1)S(1)} %layer.1) | data formatting | bytes 786432

commit v6 on v5

--- a/solution.py
+++ b/solution.py
@@ -48,10 +48,12 @@
 
 
 def layer(x_hbm, ga_hbm, gm_hbm, turn_hbm, wq_hbm, wo_hbm, wg_hbm, wu_hbm, wd_hbm, k_hbm, v_hbm, out_ref,
-          x_ref, ga_ref, gm_ref, turn_ref, kbuf, vbuf, wq, wo, wg, wu, wd, qblk, sbuf, wbuf, seen, bbuf, hid, own, part1, part2, recv1, recv2, hbuf, ybuf,
-          ksem, vsem, lastsem, wsem, send_sem, recv_sem):
+          x_ref, ga_ref, gm_ref, gain_m, turn_ref, kbuf, vbuf, wq, wo, wg, wu, wd, qblk, sbuf, wbuf, seen, bbuf, hid, own, part1, part2, recv1, recv2, hbuf, ybuf,
+          ksem, vsem, wsem, send_sem, recv_sem):
     me = lax.axis_index("tp")
     mx, my, mc = me // 4, lax.rem(me // 2, 2), lax.rem(me, 2)
+
+    here = me >= 0
 
     def chip(k):
         return 2 * lax.rem(mx + k // 2, 2) + lax.rem(my + k % 2, 2)
@@ -88,19 +90,22 @@
     last = []
     for n in range(U // ULAST):
         places = pl.ds(n * ULAST, ULAST)
-        last.append(pltpu.make_async_copy(v_hbm.at[pl.ds(B - Q, Q), places], vbuf.at[(G - 1) % VS, :, places], lastsem.at[n]))
+        last.append(pltpu.make_async_copy(v_hbm.at[pl.ds(B - Q, Q), places], vbuf.at[(G - 1) % VS, :, places], ksem.at[n] if n < NS else wsem.at[4]))
+
+    def arrivals(c, stage):
+        return len(PARTS) * (stage % 2) + c
 
     def scatter(c, stage, rows, src, dst, s):
-        return pltpu.make_async_remote_copy(src.at[at(s), rows], dst.at[s, rows], send_sem.at[stage], recv_sem.at[c, stage],
+        return pltpu.make_async_remote_copy(src.at[at(s), rows], dst.at[s, rows], send_sem, recv_sem.at[arrivals(c, stage)],
                                             device_id={"tp": at(s)}, device_id_type=MESH)
 
     def gather(c, stage, rows, buf, s):
-        return pltpu.make_async_remote_copy(buf.at[me, rows], buf.at[me, rows], send_sem.at[stage], recv_sem.at[c, stage],
+        return pltpu.make_async_remote_copy(buf.at[me, rows], buf.at[me, rows], send_sem, recv_sem.at[arrivals(c, stage)],
                                             device_id={"tp": at(s)}, device_id_type=MESH)
 
     def all_seven(c, stage, rows, buf):
         seven = buf.at[pl.ds(1, N - 1), rows]
-        return pltpu.make_async_remote_copy(seven, seven, send_sem.at[stage], recv_sem.at[c, stage],
+        return pltpu.make_async_remote_copy(seven, seven, send_sem, recv_sem.at[arrivals(c, stage)],
                                             device_id={"tp": at(1)}, device_id_type=MESH)
 
     others = (6, 7, 4, 5, 2, 3, 1)
@@ -124,6 +129,7 @@
         wide = x_ref[...].astype(F32)
         scale = lax.rsqrt(jnp.mean(wide * wide, -1, keepdims=True) + 1e-6)
         a = (wide * scale * row(ga_ref[...].astype(F32))).astype(BF16)
+        gain_m[...] = row(gm_ref[...].astype(F32))
         loads["wq"].wait()
         kcopy(1, 1).start()
         kcopy(2, 2).start()
@@ -224,11 +230,11 @@
 
     def across(k):
         block = ybuf.at[2 * chip(k) + mc, group_rows(0)]
-        return pltpu.make_async_remote_copy(block, block, send_sem.at[3], recv_sem.at[2, 3], device_id={"tp": at(1)}, device_id_type=MESH)
+        return pltpu.make_async_remote_copy(block, block, send_sem, recv_sem.at[2], device_id={"tp": at(1)}, device_id_type=MESH)
 
     def some(n, c, stage, rows, buf):
         blocks = buf.at[pl.ds(0, n), rows]
-        return pltpu.make_async_remote_copy(blocks, blocks, send_sem.at[stage], recv_sem.at[c, stage],
+        return pltpu.make_async_remote_copy(blocks, blocks, send_sem, recv_sem.at[arrivals(c, stage)],
                                             device_id={"tp": at(1)}, device_id_type=MESH)
 
     def norm2(c):
@@ -239,9 +245,8 @@
             t = hbuf[j, rows].astype(F32)
             squares += jnp.sum(t * t, -1, keepdims=True)
         scale = lax.rsqrt(squares * (1.0 / D) + 1e-6)
-        gain = row(gm_ref[...].astype(F32))
         for j in range(N):
-            bbuf[rows, j * W : (j + 1) * W] = (hbuf[j, rows].astype(F32) * scale * gain[:, j * W : (j + 1) * W]).astype(BF16)
+            bbuf[rows, j * W : (j + 1) * W] = (hbuf[j, rows].astype(F32) * scale * gain_m[:, j * W : (j + 1) * W]).astype(BF16)
 
     def hidden(c, first, width):
         rows, cols = group_rows(c), pl.ds(first, width)
@@ -307,8 +312,11 @@
     vcopy(G - LEAD, (G - LEAD) % VS).start()
     arrive(G - LEAD - 2)
     attended(G - LEAD - 2)
-    with jax.named_scope("finish1"):
-        finish(1)
+    @pl.when(here)
+    def _():
+        with jax.named_scope("finish1"):
+            finish(1)
+
     ahead(G - LEAD - 2)
     vcopy(G - LEAD + 1, (G - LEAD + 1) % VS).start()
     with jax.named_scope("arrive12"):
@@ -320,8 +328,11 @@
     with jax.named_scope("v13"):
         vcopy(G - LEAD, (G - LEAD) % VS).wait()
     attended(G - LEAD)
-    with jax.named_scope("r11"):
-        reduce1(1)
+    @pl.when(here)
+    def _():
+        with jax.named_scope("r11"):
+            reduce1(1)
+
     with jax.named_scope("v14"):
         vcopy(G - LEAD + 1, (G - LEAD + 1) % VS).wait()
     attended(G - LEAD + 1)
@@ -337,8 +348,11 @@
             copy.wait()
         o += values((G - 1) % VS, wbuf.at[(G - 1) % 2], n * ULAST, ULAST)
     keep(G - 1, o)
-    with jax.named_scope("f2"):
-        finish(2)
+    @pl.when(here)
+    def _():
+        with jax.named_scope("f2"):
+            finish(2)
+
     with jax.named_scope("n0"):
         norm2(0)
     with jax.named_scope("n01"):
@@ -346,27 +360,48 @@
     with jax.named_scope("h00"):
         both_halves(0).wait()
         hidden(0, 0 * half, half)
-    with jax.named_scope("r12"):
-        reduce1(2)
+    @pl.when(here)
+    def _():
+        with jax.named_scope("r12"):
+            reduce1(2)
+
     with jax.named_scope("h01"):
         both_halves(1).wait()
         hidden(0, 1 * half, half)
-    with jax.named_scope("d0"):
-        down(0)
-    with jax.named_scope("n1"):
-        norm2(2)
+    @pl.when(here)
+    def _():
+        with jax.named_scope("d0"):
+            down(0)
+
+    @pl.when(here)
+    def _():
+        with jax.named_scope("n1"):
+            norm2(2)
+
     with jax.named_scope("h1"):
         hidden(1, 0, HID)
-    with jax.named_scope("d1"):
-        down(1)
-    with jax.named_scope("r20"):
-        reduce2(0)
-    with jax.named_scope("r21"):
-        reduce2(1)
-    with jax.named_scope("across"):
-        some(N // 2 - 1, 0, 3, group_rows(0), ybuf).wait_recv()
-        for k in (3, 2, 1):
-            across(k).start()
+    @pl.when(here)
+    def _():
+        with jax.named_scope("d1"):
+            down(1)
+
+    @pl.when(here)
+    def _():
+        with jax.named_scope("r20"):
+            reduce2(0)
+
+    @pl.when(here)
+    def _():
+        with jax.named_scope("r21"):
+            reduce2(1)
+
+    @pl.when(here)
+    def _():
+        with jax.named_scope("across"):
+            some(N // 2 - 1, 0, 3, group_rows(0), ybuf).wait_recv()
+            for k in (3, 2, 1):
+                across(k).start()
+
 
     def put(c):
         rows = group_rows(c)
@@ -374,14 +409,14 @@
             out_ref[rows, j * W : (j + 1) * W] = ybuf[j, rows]
 
     with jax.named_scope("out0"):
-        some(N // 2, 2, 3, group_rows(0), ybuf).wait_recv()
+        some(N // 2, 2, 0, group_rows(0), ybuf).wait_recv()
     put(0)
     with jax.named_scope("out1"):
         all_seven(1, 3, group_rows(1), ybuf).wait_recv()
     put(1)
     with jax.named_scope("sent"):
-        for stage, buf in enumerate((part1, hbuf, part2, ybuf)):
-            all_seven(0, stage, pl.ds(0, B), buf).wait_send()
+        sent = wg.at[pl.ds(0, 4 * (N - 1) * B * W // HID)]
+        pltpu.make_async_remote_copy(sent, sent, send_sem, recv_sem.at[0], device_id={"tp": at(1)}, device_id_type=MESH).wait_send()
 
 
 def solution(mesh):
@@ -397,6 +432,7 @@
                 pltpu.VMEM((B, D), BF16),
                 pltpu.VMEM((D // 128, 128), BF16),
                 pltpu.VMEM((D // 128, 128), BF16),
+                pltpu.VMEM((1, D), F32),
                 pltpu.VMEM((2, HEAD), F32),
                 pltpu.VMEM((NS, Q, U, HEAD), BF16),
                 pltpu.VMEM((VS, Q, U, HEAD), BF16),
@@ -415,10 +451,9 @@
                 *[pltpu.VMEM((N, B, W), BF16)] * 6,
                 pltpu.SemaphoreType.DMA((NS,)),
                 pltpu.SemaphoreType.DMA((VS,)),
-                pltpu.SemaphoreType.DMA((U // ULAST,)),
                 pltpu.SemaphoreType.DMA((5,)),
-                pltpu.SemaphoreType.DMA((4,)),
-                pltpu.SemaphoreType.DMA((len(PARTS), 4)),
+                pltpu.SemaphoreType.DMA,
+                pltpu.SemaphoreType.DMA((2 * len(PARTS),)),
             ],
             compiler_params=pltpu.CompilerParams(collective_id=0, has_side_effects=True, vmem_limit_bytes=60 * 2**20),
             name="layer",

time: 61.2 us -> 60.7 us (level)
  no operation moved by 1% of the time
where the time goes in v6:
time: 60.7 us; the launch traced here: 60.6 us
  Pallas kernels  59.9 us (99%)
  local copies, waits for them, and re-layouts  0.75 us (1%)
    pallas_call x1, Pallas kernels, step(): pl.pallas_call(layer, out_shape=pltpu.VMEM((B, D), BF16), in_specs=[any_]...  59.9 us

profile of v6, /device:TPU:0, one launch (start us, length us, event | category | flops | bytes accessed | tf_op | source)
XLA Modules:
  0.0 60.6 jit_solution(12826244964769986804)
XLA Ops:
  0.0 59.9 %layer.1 = bf16[64,3072]{1,0:T(8,128)(2,1)S(1)} custom-call(bf16[64,3072]{1,0:T(8,128)(2,1)} %x_hbm.1, bf16[24,128]{1,0:T(8,128)(2,1)} %bitcast.4, bf16[24,128]{1,0:T(8,128)(2,1)} %bitcast.5, f32[2,128]{1,0:T(2,128)} %constant.2.clone.turn_hbm, bf16[3072,384]{1,0:T(8,128)(2,1)} %wq_hbm.1, bf16[384,3072]{1,0:T(8,128)(2,1)} %wo_hbm.1, ...), custom_call_target="tpu_custom_call" | custom-call | tf_op jit(solution)/shard_map/layer/pallas_call | solution.py:426
  59.9 0.7 %copy.13 = bf16[64,3072]{1,0:T(8,128)(2,1)} copy(bf16[64,3072]{1,0:T(8,128)(2,1)S(1)} %layer.1) | data formatting | bytes 786432
